TPU v7x, 32 devices: a whole 2x2x4 slice. The times are simulated.
32 devices in a mesh: tok: 4 (over y, core), cache: 8 (over z, x).
Axes of the slice: x: 2, y: 2, z: 4, core: 2. Of those that a mesh axis runs over, the one named last changes fastest.
Arguments:
- queries_one: bfloat16 [64, 6, 128, 576], P('cache', None, 'tok'), may hold values from -100 to 100
- keys_one: bfloat16 [64, 6, 576], P('cache'), may hold values from -12 to 12
- queries_two: bfloat16 [64, 6, 128, 576], P('cache', None, 'tok'), may hold values from -100 to 100
- keys_two: bfloat16 [64, 6, 576], P('cache'), may hold values from -12 to 12
- latent_cache: bfloat16 [64, 640, 576], P('cache'), may hold values from -8 to 8
- cached_len: int32 [64], P('cache'), may hold values from 80 to 640
- first_owner: int32 [64], P('cache'), may hold values from 0 to 7, as said below
- new_owner: int32 [64], P('cache'), may hold values from 0 to 7, as said below
- accepted: int32 [64], P('cache'), may hold values from 1 to 6
Outputs:
- first_out: bfloat16 [64, 6, 128, 512], P('cache', None, 'tok')
- second_out: bfloat16 [64, 6, 128, 512], P('cache', None, 'tok')
- arrived_cache: bfloat16 [32, 640, 576], P('cache')
Inputs may be any that keep to these rules, and one draw needn't show every extreme that they name: `first_owner`: row j of a device's 8 draft rows is the request whose cache lies in slot j of the named cache device in round one; the rows of one device name every cache device exactly once, and every slot is named by exactly one row. `new_owner`: each slot's cache keeps its position j in round two. On every device the same half of the positions j name another device and the rest the device itself; the other devices that one device names are distinct, and every device receives exactly one cache into each slot that it gives up. The round-two devices of one device's draft rows name no cache device more than 2 times, and on every device some cache device exactly 2 times.
All inputs are finite; a program needn't handle non-finite values.
Results may differ from a plain program's by a relative error of at most 0.0032.
Values may be sent and summed in bfloat16 or wider, within the bound.
No kernel may reach another device: no remote copies, remote signals or barrier semaphores. Data moves between devices by JAX's collectives and lax.ppermute only.
A program may use at most 128 MiB of HBM per device.

v0:
```python
import jax
import jax.numpy as jnp
from jax import lax
from jax.sharding import PartitionSpec as P

LAT = 512


score_factor = 192.0 ** (-0.5)


def attend(queries, cache_rows, length, extra_keys, extra_mask):
    near_score = (
        jnp.einsum("srhw,scw->srhc", queries, cache_rows, preferred_element_type=jnp.float32)
        * score_factor
    )
    places = jnp.arange(cache_rows.shape[1], dtype=jnp.int32)
    near_score = jnp.where(
        places[None, None, None, :] < length[:, None, None, None], near_score, -jnp.inf
    )
    own_score = (
        jnp.einsum("srhw,sew->srhe", queries, extra_keys, preferred_element_type=jnp.float32)
        * score_factor
    )
    own_score = jnp.where(extra_mask[:, :, None, :], own_score, -jnp.inf)
    row_max = jnp.maximum(jnp.max(near_score, axis=-1), jnp.max(own_score, axis=-1))
    near_weight = jnp.exp(near_score - row_max[..., None])
    own_weight = jnp.exp(own_score - row_max[..., None])
    denominator = jnp.sum(near_weight, axis=-1) + jnp.sum(own_weight, axis=-1)
    mixture = jnp.einsum(
        "srhc,scl->srhl",
        near_weight.astype(jnp.bfloat16),
        cache_rows[:, :, :LAT],
        preferred_element_type=jnp.float32,
    )
    mixture = mixture + jnp.einsum(
        "srhe,sel->srhl",
        own_weight.astype(jnp.bfloat16),
        extra_keys[:, :, :LAT],
        preferred_element_type=jnp.float32,
    )
    return (mixture / denominator[..., None]).astype(jnp.bfloat16)


def first_match(id_table, wanted):
    hit_table = id_table[None, :] == wanted[:, None]
    return (jnp.argmax(hit_table, axis=1), jnp.any(hit_table, axis=1))


def local(
    queries_one,
    keys_one,
    queries_two,
    keys_two,
    latent_cache,
    cached_len,
    first_owner,
    new_owner,
    accepted,
):
    peer_count = lax.axis_size("cache")
    my_index = lax.axis_index("cache")
    columns = jnp.arange(peer_count, dtype=jnp.int32)
    draft_rows = queries_one.shape[1]
    row_ids = jnp.arange(draft_rows, dtype=jnp.int32)
    causal = row_ids[:, None] >= row_ids[None, :]
    both_keys = jnp.concatenate([keys_one, keys_two], axis=1)
    pick_one, unused_one = first_match(first_owner, columns)
    sent_queries = jnp.take(queries_one, pick_one, axis=0)
    sent_keys = jnp.take(keys_one, pick_one, axis=0)
    got_queries, got_keys, got_col = (
        lax.all_to_all(sent_queries, "cache", split_axis=0, concat_axis=0, tiled=True),
        lax.all_to_all(sent_keys, "cache", split_axis=0, concat_axis=0, tiled=True),
        lax.all_to_all(pick_one, "cache", split_axis=0, concat_axis=0, tiled=True),
    )
    order_one, unused_two = first_match(got_col, columns)
    mask_one = jnp.broadcast_to(causal, (peer_count, draft_rows, draft_rows))
    out_slot = attend(
        jnp.take(got_queries, order_one, axis=0),
        latent_cache,
        cached_len,
        jnp.take(got_keys, order_one, axis=0),
        mask_one,
    )
    out_src = jnp.take(out_slot, got_col, axis=0)
    back_out = lax.all_to_all(out_src, "cache", split_axis=0, concat_axis=0, tiled=True)
    first_out = jnp.take(back_out, first_owner, axis=0)
    moving = new_owner != my_index
    move_hits = (new_owner[None, :] == columns[:, None]) & moving[None, :]
    pick_move = jnp.argmax(move_hits, axis=1)
    sent_any = jnp.any(move_hits, axis=1)
    sent_col = jnp.where(sent_any, pick_move, -1)
    sent_len = jnp.take(cached_len, pick_move, axis=0)
    outgoing = jnp.take(latent_cache, pick_move, axis=0)
    share = latent_cache.shape[1] // lax.axis_size("tok")
    piece = lax.dynamic_slice_in_dim(outgoing, lax.axis_index("tok") * share, share, 1)
    came_part, came_col, came_len = (
        lax.all_to_all(piece, "cache", split_axis=0, concat_axis=0, tiled=True),
        lax.all_to_all(sent_col, "cache", split_axis=0, concat_axis=0, tiled=True),
        lax.all_to_all(sent_len, "cache", split_axis=0, concat_axis=0, tiled=True),
    )
    came = lax.all_gather(came_part, "tok", axis=1, tiled=True)
    arrival_src, unused_three = first_match(came_col, columns)
    moved_cols = jnp.nonzero(moving, size=peer_count // 2)[0].astype(jnp.int32)
    arrived_cache = jnp.take(came, jnp.take(arrival_src, moved_cols, axis=0), axis=0)
    again_queries = jnp.take(queries_two, pick_one, axis=0)
    again_keys = jnp.take(both_keys, pick_one, axis=0)
    again_accept = jnp.take(accepted, pick_one, axis=0)
    got3_queries, got3_keys, got3_accept = (
        lax.all_to_all(again_queries, "cache", split_axis=0, concat_axis=0, tiled=True),
        lax.all_to_all(again_keys, "cache", split_axis=0, concat_axis=0, tiled=True),
        lax.all_to_all(again_accept, "cache", split_axis=0, concat_axis=0, tiled=True),
    )
    accept_slot = jnp.take(got3_accept, order_one, axis=0)
    kept_rows = jnp.broadcast_to(
        row_ids[None, None, :] < accept_slot[:, None, None], (peer_count, draft_rows, draft_rows)
    )
    mask_two = jnp.concatenate([kept_rows, mask_one], axis=2)
    out_again = attend(
        jnp.take(got3_queries, order_one, axis=0),
        latent_cache,
        cached_len,
        jnp.take(got3_keys, order_one, axis=0),
        mask_two,
    )
    again_src = jnp.take(out_again, got_col, axis=0)
    back_again = lax.all_to_all(again_src, "cache", split_axis=0, concat_axis=0, tiled=True)
    second_out = jnp.take(back_again, first_owner, axis=0)
    return (first_out, second_out, arrived_cache)


def solution(mesh):
    placed = (
        P("cache", None, "tok", None),
        P("cache", None, None),
        P("cache", None, "tok", None),
        P("cache", None, None),
        P("cache", None, None),
        P("cache"),
        P("cache"),
        P("cache"),
        P("cache"),
    )
    return jax.shard_map(
        local,
        mesh=mesh,
        in_specs=placed,
        out_specs=(
            P("cache", None, "tok", None),
            P("cache", None, "tok", None),
            P("cache", None, None),
        ),
        check_vma=False,
    )
```

profile of v0, /device:TPU:0, one launch (start us, length us, event | category | flops | bytes accessed | tf_op | source)
XLA Modules:
  0.0 352.7 jit_solution(16661628441612368324)
XLA Ops:
  7.2 1.4 iota_reduce_fusion.3
  8.6 0.7 copy.36
  9.3 7.3 %all-to-all-start.1 = ((s32[8,1,1]{2,1,0:T(1,128)}), s32[8,1,1]{2,1,0:T(1,128)S(1)}, u32[]{:S(2)}, u32[]{:S(2)}) async-start(s32[8,1,1]{2,1,0:T(1,128)} %copy.36), calls=%async_computation.1 | async-start | bytes 8192 | tf_op jit(solution)/shard_map/all_to_all | solution.py:74
  16.6 1.3 convert_reduce_fusion
  17.9 0.8 fusion.39
  18.7 1.3 iota_reduce_fusion.1
  20.0 0.8 copy.40
  20.8 1.6 gather_fusion.5
  22.4 1.3 gather_fusion.11
  23.7 0.7 copy.39
  24.4 0.8 copy.41
  25.9 0.8 broadcast_select_fusion.14
  26.7 0.6 copy.37
  27.4 6.0 %all-to-all-start.5 = ((s32[8,1,1]{2,1,0:T(1,128)}), s32[8,1,1]{2,1,0:T(1,128)S(1)}, u32[]{:S(2)}, u32[]{:S(2)}) async-start(s32[8,1,1]{2,1,0:T(1,128)} %copy.39), calls=%async_computation.5 | async-start | bytes 8192 | tf_op jit(solution)/shard_map/all_to_all | solution.py:112
  33.4 6.5 %all-to-all-done.5 = s32[8,1,1]{2,1,0:T(1,128)S(1)} async-done(((s32[8,1,1]{2,1,0:T(1,128)}), s32[8,1,1]{2,1,0:T(1,128)S(1)}, u32[]{:S(2)}, u32[]{:S(2)}) %all-to-all-start.5) | async-done | bytes 64 | tf_op jit(solution)/shard_map/all_to_all | solution.py:112
  39.9 3.4 all-to-all-start.2
  43.3 6.5 %gather_fusion.1 = bf16[8,640,576]{1,2,0:T(8,128)(2,1)} fusion(bf16[8,640,576]{1,2,0:T(8,128)(2,1)} %param.23, s32[1024]{0:T(1024)S(1)} %pad_clamp_fusion.1), kind=kCustom, calls=%fused_computation.15 | custom fusion | bytes 11796512 | tf_op jit(solution)/shard_map/jit(_take)/gather | solution.py:94
  50.2 5.5 %all-to-all-start.6 = ((bf16[8,12,576]{2,1,0:T(8,128)(2,1)}), bf16[8,12,576]{2,1,0:T(8,128)(2,1)S(1)}, u32[]{:S(2)}, u32[]{:S(2)}) async-start(bf16[8,12,576]{2,1,0:T(8,128)(2,1)} %broadcast_select_fusion.14), calls=%async_computation.6 | async-start | bytes 327680 | tf_op jit(solution)/shard_map/all_to_all | solution.py:111
  55.7 4.8 %dynamic-slice_select_fusion = bf16[8,160,576]{1,2,0:T(8,128)(2,1)} fusion(bf16[8,640,576]{1,2,0:T(8,128)(2,1)} %gather_fusion.1, s32[]{:T(128)S(6)} %select_n.214, pred[8]{0:T(512)(128)(4,1)S(1)} %compare_and_fusion.4), kind=kLoop, calls=%fused_computation.41 | loop fusion | flops 737280 | bytes 2949132 | tf_op jit(solution)/shard_map/jit(_take)/select_n | solution.py:94
  60.5 4.0 %copy.43 = bf16[8,160,576]{2,1,0:T(8,128)(2,1)} copy(bf16[8,160,576]{1,2,0:T(8,128)(2,1)} %dynamic-slice_select_fusion) | data formatting | bytes 2949120 | tf_op jit(solution)/shard_map/dynamic_slice | solution.py:96
  64.5 6.0 %all-to-all-start.9 = ((bf16[8,160,576]{2,1,0:T(8,128)(2,1)}), bf16[8,160,576]{2,1,0:T(8,128)(2,1)}, u32[]{:S(2)}, u32[]{:S(2)}) async-start(bf16[8,160,576]{2,1,0:T(8,128)(2,1)} %copy.43), calls=%async_computation.9 | async-start | bytes 3276800 | tf_op jit(solution)/shard_map/all_to_all | solution.py:98
  70.5 2.1 gather_fusion.9
  72.5 3.8 %gather_fusion.3 = bf16[8,6,32,576]{3,2,1,0:T(8,128)(2,1)} fusion(bf16[8,6,32,576]{3,2,1,0:T(8,128)(2,1)} %param.19, s32[1024]{0:T(1024)S(1)} %pad_clamp_fusion.6), kind=kCustom, calls=%fused_computation.clone | custom fusion | bytes 3538976 | tf_op jit(solution)/shard_map/jit(_take)/gather | solution.py:69
  76.3 4.0 %broadcast_select_fusion.3 = (bf16[8,6,32,576]{3,2,1,0:T(8,128)(2,1)}, bf16[8,6,32,576]{3,2,1,0:T(8,128)(2,1)}) fusion(bf16[8,6,32,576]{3,2,1,0:T(8,128)(2,1)S(1)} %copy-done.4, pred[8]{0:T(512)(128)(4,1)S(1)} %get-tuple-element.25, bf16[8,6,32,576]{3,2,1,0:T(8,128)(2,1)} %gather_fusion.3), kind=kLoop, calls=%fused_computation.50 | loop fusion | flops 1769472 | bytes 7077896 | tf_op jit(solution)/shard_map/jit(_take)/select_n | solution.py:106
  80.2 26.1 %all-to-all-done.9 = bf16[8,160,576]{2,1,0:T(8,128)(2,1)} async-done(((bf16[8,160,576]{2,1,0:T(8,128)(2,1)}), bf16[8,160,576]{2,1,0:T(8,128)(2,1)}, u32[]{:S(2)}, u32[]{:S(2)}) %all-to-all-start.9) | async-done | bytes 1474592 | tf_op jit(solution)/shard_map/all_to_all | solution.py:98
  106.4 3.7 %all-to-all-start = ((bf16[8,6,32,576]{3,2,1,0:T(8,128)(2,1)}), bf16[8,6,32,576]{3,2,1,0:T(8,128)(2,1)S(1)}, u32[]{:S(2)}, u32[]{:S(2)}) async-start(bf16[8,6,32,576]{3,2,1,0:T(8,128)(2,1)} %get-tuple-element.33), calls=%async_computation | async-start | bytes 3932160 | tf_op jit(solution)/shard_map/all_to_all | solution.py:72
  110.1 0.7 copy.42
  110.9 44.7 %all-to-all-done = bf16[8,6,32,576]{3,2,1,0:T(8,128)(2,1)S(1)} async-done(((bf16[8,6,32,576]{3,2,1,0:T(8,128)(2,1)}), bf16[8,6,32,576]{3,2,1,0:T(8,128)(2,1)S(1)}, u32[]{:S(2)}, u32[]{:S(2)}) %all-to-all-start) | async-done | bytes 1769504 | tf_op jit(solution)/shard_map/all_to_all | solution.py:72
  155.5 1.3 copy-done.3
  156.9 4.3 %all-to-all-start.4 = ((bf16[8,6,32,576]{3,2,1,0:T(8,128)(2,1)}), bf16[8,6,32,576]{3,2,1,0:T(8,128)(2,1)}, u32[]{:S(2)}, u32[]{:S(2)}) async-start(bf16[8,6,32,576]{3,2,1,0:T(8,128)(2,1)} %get-tuple-element.32), calls=%async_computation.4 | async-start | bytes 3932160 | tf_op jit(solution)/shard_map/all_to_all | solution.py:110
  161.7 0.6 iota_reduce_fusion.2
  162.4 0.6 gather_fusion.12
  164.3 0.7 broadcast_select_fusion.15
  165.7 3.2 copy.44
  168.9 2.5 gather_fusion.4
  171.4 2.4 fusion.55
  173.8 7.2 %fusion.2 = f32[8,6,32,640]{3,2,1,0:T(8,128)} fusion(bf16[8,640,576]{1,2,0:T(8,128)(2,1)} %param.23, bf16[8,6,32,576]{3,2,1,0:T(8,128)(2,1)S(1)} %gather_fusion.4, pred[8]{0:T(512)(128)(4,1)S(1)} %get-tuple-element.23), kind=kOutput, calls=%fused_computation.20 | convolution fusion | flops 1133346816 | bytes 11599880 | tf_op jit(solution)/shard_map/srhw,scw->srhc/dot_general | solution.py:14
  181.0 25.3 %all-to-all-done.4 = bf16[8,6,32,576]{3,2,1,0:T(8,128)(2,1)} async-done(((bf16[8,6,32,576]{3,2,1,0:T(8,128)(2,1)}), bf16[8,6,32,576]{3,2,1,0:T(8,128)(2,1)}, u32[]{:S(2)}, u32[]{:S(2)}) %all-to-all-start.4) | async-done | bytes 1769504 | tf_op jit(solution)/shard_map/all_to_all | solution.py:110
  206.2 3.6 %all-to-all-start.8 = ((s32[8,1,1]{2,1,0:T(1,128)}), s32[8,1,1]{2,1,0:T(1,128)S(1)}, u32[]{:S(2)}, u32[]{:S(2)}) async-start(s32[8,1,1]{2,1,0:T(1,128)} %copy.42), calls=%async_computation.8 | async-start | bytes 8192 | tf_op jit(solution)/shard_map/all_to_all | solution.py:99
  209.8 2.4 gather_fusion.10
  212.3 1.7 fusion.54
  214.1 6.5 %fusion.11 = (f32[8,6,32]{2,1,0:T(8,128)S(1)}, f32[8,6,32]{2,1,0:T(8,128)S(1)}, f32[8,6,32,640]{3,2,1,0:T(8,128)S(1)}) fusion(pred[8,640]{1,0:T(8,128)(4,1)S(1)} %iota_compare_fusion, f32[8,6,32,640]{3,2,1,0:T(8,128)} %fusion.2, bf16[8,640,576]{1,2,0:T(8,128)(2,1)} %param.23, bf16[8,6,32,576]{3,2,1,0:T(8,128)(2,1)S(1)} %gather_fusion.10, ...), kind=kOutput, calls=%fused_computation.33 | convolution fusion | flops 1139241984 | bytes 15549448 | tf_op jit(solution)/shard_map/srhw,scw->srhc/dot_general | solution.py:14
  220.6 2.1 fusion.14
  222.9 2.2 fusion.4
  225.1 0.6 divide_convert_fusion
  225.8 0.6 gather_fusion.15
  226.8 5.7 %fusion.6 = f32[8,6,32,512]{3,2,1,0:T(8,128)S(1)} fusion(bf16[8,640,576]{1,2,0:T(8,128)(2,1)} %param.23, f32[8,6,32,640]{3,2,1,0:T(8,128)} %fusion.2, f32[8,6,32]{2,1,0:T(8,128)S(1)} %max.14, pred[8,640]{1,0:T(8,128)(4,1)S(1)} %iota_compare_fusion), kind=kOutput, calls=%fused_computation.24 | convolution fusion | flops 1010565120 | bytes 12332032 | tf_op jit(solution)/shard_map/srhc,scl->srhl/dot_general | solution.py:30
  232.6 0.7 divide_convert_fusion.1
  233.3 1.8 gather_fusion.7
  235.1 2.9 broadcast_select_fusion.7
  237.9 42.4 %all_to_all.65 = bf16[8,6,32,512]{3,2,1,0:T(8,128)(2,1)S(1)} all-to-all(bf16[8,6,32,512]{3,2,1,0:T(8,128)(2,1)S(1)} %get-tuple-element.30), channel_id=1, replica_groups=mesh['tok'=4,'cache'=8] {'cache'}, dimensions={0} | all-to-all | bytes 3145728 | tf_op jit(solution)/shard_map/all_to_all | solution.py:127
  280.4 3.7 %all-to-all-start.3 = ((bf16[8,6,32,512]{3,2,1,0:T(8,128)(2,1)}), bf16[8,6,32,512]{3,2,1,0:T(8,128)(2,1)S(1)}, u32[]{:S(2)}, u32[]{:S(2)}) async-start(bf16[8,6,32,512]{3,2,1,0:T(8,128)(2,1)} %get-tuple-element.31), calls=%async_computation.3 | async-start | bytes 3145728 | tf_op jit(solution)/shard_map/all_to_all | solution.py:86
  285.1 0.6 fusion.56
  286.1 0.6 iota_reduce_fusion
  286.7 0.6 gather_fusion
  287.3 0.6 fusion.43
  288.0 0.6 compare_and_fusion.5
  288.6 1.8 gather_fusion.16
  290.4 30.2 %all-to-all-done.3 = bf16[8,6,32,512]{3,2,1,0:T(8,128)(2,1)S(1)} async-done(((bf16[8,6,32,512]{3,2,1,0:T(8,128)(2,1)}), bf16[8,6,32,512]{3,2,1,0:T(8,128)(2,1)S(1)}, u32[]{:S(2)}, u32[]{:S(2)}) %all-to-all-start.3) | async-done | bytes 1572896 | tf_op jit(solution)/shard_map/all_to_all | solution.py:86
  320.7 1.8 gather_fusion.8
  322.5 3.4 broadcast_select_fusion.5
  325.9 10.8 %copy.45 = bf16[8,640,576]{1,2,0:T(8,128)(2,1)} copy(bf16[8,640,576]{2,0,1:T(8,128)(2,1)} %all-gather.2.cloned.1.call-done) | data formatting | bytes 11796480 | tf_op jit(solution)/shard_map/all_gather | solution.py:102
  336.7 5.3 %gather_fusion.2 = bf16[4,640,576]{1,2,0:T(8,128)(2,1)} fusion(bf16[8,640,576]{1,2,0:T(8,128)(2,1)} %copy.45, s32[1024]{0:T(1024)S(1)} %pad_clamp_fusion), kind=kCustom, calls=%fused_computation.16 | custom fusion | bytes 5898256 | tf_op jit(solution)/shard_map/jit(_take)/gather | solution.py:105
  342.0 3.8 %broadcast_select_fusion = bf16[4,640,576]{1,2,0:T(8,128)(2,1)} fusion(bf16[4,640,576]{1,2,0:T(8,128)(2,1)} %gather_fusion.2, pred[4]{0:T(512)(128)(4,1)S(1)} %compare_and_fusion.5), kind=kLoop, calls=%fused_computation.40 | loop fusion | flops 1474560 | bytes 5898244 | tf_op jit(solution)/shard_map/jit(_take)/select_n | solution.py:105
  (81 shorter events, 5.6 us)
Async XLA Ops:
  7.2 63.3 %copy-start = (bf16[8,6,32,576]{3,2,1,0:T(8,128)(2,1)S(1)}, bf16[8,6,32,576]{3,2,1,0:T(8,128)(2,1)}, u32[]{:S(2)}) copy-start(bf16[8,6,32,576]{3,2,1,0:T(8,128)(2,1)} %param.21) | copy-start | bytes 5308420
  9.3 18.1 %all-to-all-start.1 = ((s32[8,1,1]{2,1,0:T(1,128)}), s32[8,1,1]{2,1,0:T(1,128)S(1)}, u32[]{:S(2)}, u32[]{:S(2)}) async-start(s32[8,1,1]{2,1,0:T(1,128)} %copy.36), calls=%async_computation.1 | async-start | bytes 8192 | tf_op jit(solution)/shard_map/all_to_all | solution.py:74
  17.9 4.5 %copy-start.8 = (pred[8]{0:T(512)(128)(4,1)}, pred[8]{0:T(512)(128)(4,1)S(1)}, u32[]{:S(2)}) copy-start(pred[8]{0:T(512)(128)(4,1)S(1)} %get-tuple-element.21) | copy-start | bytes 28
  27.4 12.5 %all-to-all-start.5 = ((s32[8,1,1]{2,1,0:T(1,128)}), s32[8,1,1]{2,1,0:T(1,128)S(1)}, u32[]{:S(2)}, u32[]{:S(2)}) async-start(s32[8,1,1]{2,1,0:T(1,128)} %copy.39), calls=%async_computation.5 | async-start | bytes 8192 | tf_op jit(solution)/shard_map/all_to_all | solution.py:112
  39.9 10.3 %all-to-all-start.2 = ((bf16[8,6,576]{2,1,0:T(8,128)(2,1)}), bf16[8,6,576]{2,1,0:T(8,128)(2,1)S(1)}, u32[]{:S(2)}, u32[]{:S(2)}) async-start(bf16[8,6,576]{2,1,0:T(8,128)(2,1)} %copy.37), calls=%async_computation.2 | async-start | bytes 163840 | tf_op jit(solution)/shard_map/all_to_all | solution.py:73
  50.2 14.3 %all-to-all-start.6 = ((bf16[8,12,576]{2,1,0:T(8,128)(2,1)}), bf16[8,12,576]{2,1,0:T(8,128)(2,1)S(1)}, u32[]{:S(2)}, u32[]{:S(2)}) async-start(bf16[8,12,576]{2,1,0:T(8,128)(2,1)} %broadcast_select_fusion.14), calls=%async_computation.6 | async-start | bytes 327680 | tf_op jit(solution)/shard_map/all_to_all | solution.py:111
  64.5 41.9 %all-to-all-start.9 = ((bf16[8,160,576]{2,1,0:T(8,128)(2,1)}), bf16[8,160,576]{2,1,0:T(8,128)(2,1)}, u32[]{:S(2)}, u32[]{:S(2)}) async-start(bf16[8,160,576]{2,1,0:T(8,128)(2,1)} %copy.43), calls=%async_computation.9 | async-start | bytes 3276800 | tf_op jit(solution)/shard_map/all_to_all | solution.py:98
  72.5 3.8 %copy-start.4 = (bf16[8,6,32,576]{3,2,1,0:T(8,128)(2,1)S(1)}, bf16[8,6,32,576]{3,2,1,0:T(8,128)(2,1)}, u32[]{:S(2)}) copy-start(bf16[8,6,32,576]{3,2,1,0:T(8,128)(2,1)} %gather_fusion.9) | copy-start | bytes 5308420
  106.4 4.4 %copy-start.11 = (s32[8]{0:T(128)S(1)}, s32[8]{0:T(128)}, u32[]{:S(2)}) copy-start(s32[8]{0:T(128)} %param.24) | copy-start | bytes 100
  106.4 49.2 %all-to-all-start = ((bf16[8,6,32,576]{3,2,1,0:T(8,128)(2,1)}), bf16[8,6,32,576]{3,2,1,0:T(8,128)(2,1)S(1)}, u32[]{:S(2)}, u32[]{:S(2)}) async-start(bf16[8,6,32,576]{3,2,1,0:T(8,128)(2,1)} %get-tuple-element.33), calls=%async_computation | async-start | bytes 3932160 | tf_op jit(solution)/shard_map/all_to_all | solution.py:72
  155.5 1.3 copy-start.3
  156.9 49.4 %all-to-all-start.4 = ((bf16[8,6,32,576]{3,2,1,0:T(8,128)(2,1)}), bf16[8,6,32,576]{3,2,1,0:T(8,128)(2,1)}, u32[]{:S(2)}, u32[]{:S(2)}) async-start(bf16[8,6,32,576]{3,2,1,0:T(8,128)(2,1)} %get-tuple-element.32), calls=%async_computation.4 | async-start | bytes 3932160 | tf_op jit(solution)/shard_map/all_to_all | solution.py:110
  161.2 164.7 %all-gather.2.cloned.1.call-start = ((), (), s32[]{:S(2)}) async-start(), calls=%async_computation.10 | async-start | bytes 8192000 | tf_op jit(solution)/shard_map/all_gather | solution.py:102
  206.2 31.7 %all-to-all-start.8 = ((s32[8,1,1]{2,1,0:T(1,128)}), s32[8,1,1]{2,1,0:T(1,128)S(1)}, u32[]{:S(2)}, u32[]{:S(2)}) async-start(s32[8,1,1]{2,1,0:T(1,128)} %copy.42), calls=%async_computation.8 | async-start | bytes 8192 | tf_op jit(solution)/shard_map/all_to_all | solution.py:99
  212.3 10.6 %slice-start = ((s8[5898240]{0:T(1024)(128)(4,1)}), s8[4194304]{0:T(1024)(128)(4,1)S(1)}, s32[]{:S(2)}) async-start(s8[5898240]{0:T(1024)(128)(4,1)} %bitcast.64), calls=%async_computation.11 | async-start | bytes 8388608
  214.0 6.6 %copy-start.2 = (f32[8,6,32,640]{3,2,1,0:T(8,128)S(1)}, f32[8,6,32,640]{3,2,1,0:T(8,128)}, u32[]{:S(2)}) copy-start(f32[8,6,32,640]{3,2,1,0:T(8,128)} %fusion.2) | copy-start | bytes 11796484
  214.1 8.8 %slice-start.1 = ((s8[5898240]{0:T(1024)(128)(4,1)}), s8[1703936]{0:T(1024)(128)(4,1)S(1)}, s32[]{:S(2)}) async-start(s8[5898240]{0:T(1024)(128)(4,1)} %bitcast.64), calls=%async_computation.12 | async-start | bytes 3407872
  225.8 0.9 copy-start.6
  226.8 5.7 %copy-start.7 = (bf16[8,6,576]{2,1,0:T(8,128)(2,1)S(1)}, bf16[8,6,576]{2,1,0:T(8,128)(2,1)}, u32[]{:S(2)}) copy-start(bf16[8,6,576]{2,1,0:T(8,128)(2,1)} %broadcast_select_fusion.15) | copy-start | bytes 165892
  233.2 1.8 copy-start.10
  280.4 3.7 %copy-start.9 = (pred[8]{0:T(512)(128)(4,1)S(1)}, pred[8]{0:T(512)(128)(4,1)}, u32[]{:S(2)}) copy-start(pred[8]{0:T(512)(128)(4,1)} %copy-done.8) | copy-start | bytes 28
  280.4 4.7 %copy-start.12 = (s32[8]{0:T(128)S(1)}, s32[8]{0:T(128)}, u32[]{:S(2)}) copy-start(s32[8]{0:T(128)} %param.25) | copy-start | bytes 100
  280.4 40.3 %all-to-all-start.3 = ((bf16[8,6,32,512]{3,2,1,0:T(8,128)(2,1)}), bf16[8,6,32,512]{3,2,1,0:T(8,128)(2,1)S(1)}, u32[]{:S(2)}, u32[]{:S(2)}) async-start(bf16[8,6,32,512]{3,2,1,0:T(8,128)(2,1)} %get-tuple-element.31), calls=%async_computation.3 | async-start | bytes 3145728 | tf_op jit(solution)/shard_map/all_to_all | solution.py:86
  290.4 32.0 %copy-start.5 = (bf16[8,6,32,512]{3,2,1,0:T(8,128)(2,1)S(1)}, bf16[8,6,32,512]{3,2,1,0:T(8,128)(2,1)}, u32[]{:S(2)}) copy-start(bf16[8,6,32,512]{3,2,1,0:T(8,128)(2,1)} %gather_fusion.16) | copy-start | bytes 4718596
  336.7 9.1 %copy-start.1 = (bf16[8,6,32,576]{3,2,1,0:T(8,128)(2,1)S(1)}, bf16[8,6,32,576]{3,2,1,0:T(8,128)(2,1)}, u32[]{:S(2)}) copy-start(bf16[8,6,32,576]{3,2,1,0:T(8,128)(2,1)} %param.21) | copy-start | bytes 5308420
Sparse Core Ops, SparseCore 0:
  169.0 48.7 all-gather.1
where the time goes:
time: 354 us; the launch traced here: 353 us
  waiting for transfers between devices  133 us (38%)
  local copies, waits for them, and re-layouts  58.4 us (16%)
  starting transfers between devices  43.5 us (12%)
  blocking collectives  42.4 us (12%)
  other arithmetic  33.4 us (9%)
  matrix products  27.1 us (8%)
  between operations  14.5 us (4%)
    all_to_all x1, waiting for transfers between devices, local(): lax.all_to_all(sent_queries, 'cache', split_axis=0, concat_axis=0, tiled=...  44.7 us
    all_to_all x1, blocking collectives, local(): lax.all_to_all(again_src, 'cache', split_axis=0, concat_axis=0, tiled=True)  42.4 us
    all_to_all x1, waiting for transfers between devices, local(): lax.all_to_all(out_src, 'cache', split_axis=0, concat_axis=0, tiled=True)  30.2 us
    all_to_all x1, waiting for transfers between devices, local(): lax.all_to_all(piece, 'cache', split_axis=0, concat_axis=0, tiled=True)  26.1 us
    all_to_all x1, waiting for transfers between devices, local(): lax.all_to_all(again_queries, 'cache', split_axis=0, concat_axis=0, tiled...  25.3 us
    dot_general x2, matrix products, attend(): jnp.einsum('srhw,scw->srhc', queries, cache_rows, preferred_element_type=...  13.7 us
    all_gather x1, local copies, waits for them, and re-layouts, local(): came = lax.all_gather(came_part, 'tok', axis=1, tiled=True)  10.8 us
    dot_general x2, matrix products, attend(): jnp.einsum('srhc,scl->srhl', near_weight.astype(jnp.bfloat16), cache_rows...  7.95 us
  transfers between devices with their start and end apart: 10, of which 6 were waited for; matrix products, arithmetic and copies ran while one was open for 27% of the time, Pallas kernels for 0%

commit v1 on v0

v1 whole, which is shorter than its diff:
```python
import functools

import jax
import jax.numpy as jnp
from jax import lax
from jax.experimental import pallas as pl
from jax.experimental.pallas import tpu as pltpu
from jax.sharding import PartitionSpec as P

LAT = 512
CORES = 2
ROWS = 16

score_factor = 192.0 ** (-0.5)
log2_e = 1.4426950408889634
ANY = pl.BlockSpec(memory_space=pl.ANY)
SMEM = pl.BlockSpec(memory_space=pltpu.SMEM)
VMEM = pl.BlockSpec(memory_space=pltpu.VMEM)


def round_up(value, step):
    return -(-value // step) * step


def take_kernel(count, pick_ref, base_ref, table_ref, out_ref, sems):
    rows = out_ref.shape[1]
    base = pl.multiple_of(base_ref[0], ROWS)
    copies = [
        pltpu.make_async_copy(
            table_ref.at[pick_ref[d], pl.ds(base, rows)], out_ref.at[d], sems.at[d]
        )
        for d in range(count)
    ]
    for copy in copies:
        copy.start()
    for copy in copies:
        copy.wait()


def take_rows(table, pick, base, rows):
    count = pick.shape[0]
    size = count * rows * table.shape[2] * table.dtype.itemsize
    return pl.pallas_call(
        functools.partial(take_kernel, count),
        out_shape=jax.ShapeDtypeStruct((count, rows, table.shape[2]), table.dtype),
        in_specs=[SMEM, SMEM, ANY],
        out_specs=VMEM,
        scratch_shapes=[pltpu.SemaphoreType.DMA((count,))],
        cost_estimate=pl.CostEstimate(flops=2 * size, bytes_accessed=2 * size, transcendentals=0),
        name="take_rows",
    )(pick, base[None], table)


def place_kernel(spans, count, starts_ref, *refs):
    parts, out_ref, bufs = refs[: len(spans)], refs[len(spans)], refs[len(spans) + 1 : -2]
    in_sems, out_sems = refs[-2:]
    loads, stores = [], []
    for p, (origin, off, rows) in enumerate(spans):
        base = pl.multiple_of(starts_ref[origin] + off, ROWS)
        for k in range(count):
            loads.append(
                pltpu.make_async_copy(parts[p].at[k], bufs[p].at[k], in_sems.at[p, k])
            )
            stores.append(
                pltpu.make_async_copy(
                    bufs[p].at[k], out_ref.at[k, pl.ds(base, rows)], out_sems.at[p, k]
                )
            )
    for load in loads:
        load.start()
    for load, store in zip(loads, stores):
        load.wait()
        store.start()
    for store in stores:
        store.wait()


def place_parts(parts, spans, starts, width):
    count, _, lanes = parts[0].shape
    dtype = parts[0].dtype
    size = count * width * lanes * dtype.itemsize
    return pl.pallas_call(
        functools.partial(place_kernel, spans, count),
        out_shape=jax.ShapeDtypeStruct((count, width, lanes), dtype),
        in_specs=[SMEM] + [ANY] * len(parts),
        out_specs=ANY,
        scratch_shapes=[pltpu.VMEM(part.shape, dtype) for part in parts]
        + [pltpu.SemaphoreType.DMA((len(parts), count))] * 2,
        cost_estimate=pl.CostEstimate(flops=2 * size, bytes_accessed=2 * size, transcendentals=0),
        name="place_parts",
    )(starts, *parts)


def attend(queries, keys_t, length, extra, extra_mask):
    scale = score_factor * log2_e
    near = jnp.dot(queries, keys_t, preferred_element_type=jnp.float32) * scale
    places = lax.broadcasted_iota(jnp.int32, (1, keys_t.shape[1]), 1)
    near = jnp.where(places < length, near, -jnp.inf)
    own = (
        lax.dot_general(
            queries, extra, (((1,), (1,)), ((), ())), preferred_element_type=jnp.float32
        )
        * scale
    )
    own = jnp.where(extra_mask, own, -jnp.inf)
    row_max = jnp.maximum(
        jnp.max(near, axis=1, keepdims=True), jnp.max(own, axis=1, keepdims=True)
    )
    near_weight = jnp.exp2(near - row_max)
    own_weight = jnp.exp2(own - row_max)
    total = jnp.sum(near_weight, axis=1, keepdims=True) + jnp.sum(
        own_weight, axis=1, keepdims=True
    )
    mixture = lax.dot_general(
        near_weight.astype(jnp.bfloat16),
        keys_t[:LAT],
        (((1,), (1,)), ((), ())),
        preferred_element_type=jnp.float32,
    )
    mixture = mixture + jnp.dot(
        own_weight.astype(jnp.bfloat16), extra[:, :LAT], preferred_element_type=jnp.float32
    )
    return (mixture * (1.0 / total)).astype(jnp.bfloat16)


def attend_kernel(spans, draft, owner_ref, length_ref, accept_ref, starts_ref, *refs):
    q1_ref, q2_ref, extra_ref = refs[:3]
    parts = refs[3 : 3 + len(spans)]
    o1_ref, o2_ref, held, sems = refs[3 + len(spans) :]
    step, steps = pl.program_id(0), pl.num_programs(0)

    def copies(r):
        for p, (origin, off, rows) in enumerate(spans):
            base = pl.multiple_of(starts_ref[origin] + off, ROWS)
            yield pltpu.make_async_copy(
                parts[p].at[owner_ref[r]], held.at[r, pl.ds(base, rows)], sems.at[r, p]
            )

    @pl.when(step == 0)
    def _():
        @pl.loop(0, steps)
        def _(r):
            for copy in copies(r):
                copy.start()

    for copy in copies(step):
        copy.wait()
    rows = q1_ref.shape[1]
    heads = rows // draft
    extra = extra_ref[0]
    row = lax.broadcasted_iota(jnp.int32, (rows, extra.shape[0]), 0)
    col = lax.broadcasted_iota(jnp.int32, (rows, extra.shape[0]), 1)
    causal_one = (col < draft) & (row >= col * heads)
    causal_two = (col >= draft) & (col < 2 * draft) & (row >= (col - draft) * heads)
    kept = (col < draft) & (col < accept_ref[step])
    keys_t = held[step]
    length = length_ref[step]
    o1_ref[0] = attend(q1_ref[0], keys_t, length, extra, causal_one)
    o2_ref[0] = attend(q2_ref[0], keys_t, length, extra, kept | causal_two)


def attend_all(q1, q2, extra, parts, spans, starts, owner, length, accepted, draft):
    reqs, rows, width = q1.shape
    positions = parts[0].shape[2]
    pieces = len(parts)
    block = lambda lanes: pl.BlockSpec((1, rows, lanes), lambda r: (r, 0, 0))
    out = jax.ShapeDtypeStruct((reqs, rows, LAT), jnp.bfloat16)
    flops = 2 * 2 * reqs * rows * positions * (width + LAT)
    return pl.pallas_call(
        functools.partial(attend_kernel, spans, draft),
        grid=(reqs,),
        out_shape=(out, out),
        in_specs=[SMEM] * 4
        + [block(width), block(width)]
        + [pl.BlockSpec((1,) + extra.shape[1:], lambda r: (r, 0, 0))]
        + [ANY] * pieces,
        out_specs=(block(LAT), block(LAT)),
        scratch_shapes=[
            pltpu.VMEM((reqs, width, positions), jnp.bfloat16),
            pltpu.SemaphoreType.DMA((reqs, pieces)),
        ],
        cost_estimate=pl.CostEstimate(
            flops=flops, bytes_accessed=reqs * width * positions * 4, transcendentals=0
        ),
        compiler_params=pltpu.CompilerParams(dimension_semantics=("arbitrary",)),
        name="attend_all",
    )(owner, length, accepted, starts, q1, q2, extra, *parts)


def local(
    queries_one,
    keys_one,
    queries_two,
    keys_two,
    latent_cache,
    cached_len,
    first_owner,
    new_owner,
    accepted,
):
    peers = lax.axis_size("cache")
    me = lax.axis_index("cache")
    groups = lax.axis_size("tok")
    group = lax.axis_index("tok")
    chips = groups // CORES
    reqs, draft, heads, width = queries_one.shape
    columns = jnp.arange(peers, dtype=jnp.int32)

    def pick(table, hits, axis):
        return jnp.sum(jnp.where(hits, table, 0), axis=axis, dtype=jnp.int32)

    def exchange(x):
        return lax.all_to_all(x, "cache", split_axis=0, concat_axis=0, tiled=True)

    owned = first_owner[None, :] == columns[:, None]
    pick_one = pick(columns[None, :], owned, 1)
    told = jnp.concatenate(
        [
            pick_one[:, None],
            jnp.broadcast_to(cached_len[None, :], (peers, reqs)),
            jnp.broadcast_to(new_owner[None, :], (peers, reqs)),
        ],
        axis=1,
    )
    heard = exchange(told)
    sent_slot = heard[:, 0]
    all_len = heard[:, 1 : 1 + reqs]
    all_new = heard[:, 1 + reqs :]
    length = pick(all_len, owned, 0)

    cache_t = jnp.swapaxes(latent_cache, 1, 2)
    share = round_up(-(-width // groups), ROWS)
    start_of = lambda t: jnp.minimum(t * share, width - share).astype(jnp.int32)
    base = start_of(group)
    chip, core = group // CORES, group % CORES
    origins = [group] + [(chip + chips - s) % chips * CORES + core for s in range(1, chips)]
    origins += [t + 1 - 2 * core for t in origins]
    starts = jnp.stack([start_of(t) for t in origins])

    def spread(part):
        held = [part]
        for s in range(1, chips):
            hop = [
                (c * CORES + k, (c + s) % chips * CORES + k)
                for c in range(chips)
                for k in range(CORES)
            ]
            held.append(lax.ppermute(part, "tok", hop))
        swap = [(t, t + 1 - 2 * (t % CORES)) for t in range(groups)]
        return held + [lax.ppermute(x, "tok", swap) for x in held]

    def cuts(count):
        size = round_up(-(-share // count), ROWS)
        return [(off, min(size, share - off)) for off in range(0, share, size)]

    draft_parts, draft_spans = [], []
    for off, rows in cuts(1):
        came = exchange(take_rows(cache_t, sent_slot, base + off, rows))
        draft_parts += spread(came)
        draft_spans += [(k, off, rows) for k in range(groups)]

    moving = new_owner != me
    sent_move = pick(columns[None, :], (new_owner[None, :] == columns[:, None]) & moving[None, :], 1)
    source = pick(columns[:, None], all_new == me, 0)
    order = jnp.cumsum(moving.astype(jnp.int32)) - 1
    moved = jnp.arange(peers // 2, dtype=jnp.int32)
    moved_source = pick(source[None, :], (order[None, :] == moved[:, None]) & moving[None, :], 1)
    move_parts, move_spans = [], []
    for off, rows in cuts(1):
        came = exchange(take_rows(cache_t, sent_move, base + off, rows))
        real = take_rows(came, moved_source, jnp.int32(0), rows)
        move_parts += spread(real)
        move_spans += [(k, off, rows) for k in range(groups)]
    arrived = place_parts(move_parts, move_spans, starts, width)

    extra = jnp.concatenate([keys_one, keys_two], axis=1)
    extra = jnp.pad(extra, ((0, 0), (0, round_up(2 * draft, ROWS) - 2 * draft), (0, 0)))
    flat = (reqs, draft * heads, width)
    first_out, second_out = attend_all(
        queries_one.reshape(flat),
        queries_two.reshape(flat),
        extra,
        draft_parts,
        draft_spans,
        starts,
        first_owner,
        length,
        accepted,
        draft,
    )
    shape = (reqs, draft, heads, LAT)
    return first_out.reshape(shape), second_out.reshape(shape), jnp.swapaxes(arrived, 1, 2)


def solution(mesh):
    placed = (
        P("cache", None, "tok", None),
        P("cache", None, None),
        P("cache", None, "tok", None),
        P("cache", None, None),
        P("cache", None, None),
        P("cache"),
        P("cache"),
        P("cache"),
        P("cache"),
    )
    return jax.shard_map(
        local,
        mesh=mesh,
        in_specs=placed,
        out_specs=(
            P("cache", None, "tok", None),
            P("cache", None, "tok", None),
            P("cache", None, None),
        ),
        check_vma=False,
    )
```

time: 354 us -> 142 us (0.40)
  local copies, waits for them, and re-layouts: 58.4 us -> 3.35 us
  waiting for transfers between devices: 133 us -> 84.1 us
  blocking collectives: 42.4 us -> 0 us
  Pallas kernels: 0 us -> 30.3 us
  other arithmetic: 33.4 us -> 4.94 us
  matrix products: 27.1 us -> 0 us
  starting transfers between devices: 43.5 us -> 18.2 us
  between operations: 14.5 us -> 0.79 us
    all_to_all x9 -> x3, waiting for transfers between devices: 133 us -> 68 us  [exchange(): return lax.all_to_all(x, 'cache', split_axis=0, concat_axis=0, tiled=True)]
    all_to_all x1 -> x0, blocking collectives: 42.4 us -> none  [local(): lax.all_to_all(again_src, 'cache', split_axis=0, concat_axis=0, tiled=True)]
    gather x17 -> x0, local copies, waits for them, and re-layouts: 34.4 us -> none  [the longest x1 6.47 us: local(): outgoing = jnp.take(latent_cache, pick_move, axis=0)]
    pallas_call x0 -> x5, Pallas kernels: none -> 30.3 us  [the longest x1 17.2 us: attend_all(): pl.pallas_call(functools.partial(attend_kernel, spans, draft), grid=(reqs...]
    all_to_all x9 -> x3, starting transfers between devices: 43.5 us -> 14.4 us  [exchange(): return lax.all_to_all(x, 'cache', split_axis=0, concat_axis=0, tiled=True)]
    dot_general x8 -> x0, matrix products: 27.1 us -> none  [the longest x2 13.7 us: attend(): jnp.einsum('srhw,scw->srhc', queries, cache_rows, preferred_element_type=...]
    select_n x18 -> x0, other arithmetic: 22 us -> none  [the longest x1 4.8 us: local(): outgoing = jnp.take(latent_cache, pick_move, axis=0)]
    ppermute x0 -> x6, waiting for transfers between devices: none -> 16.1 us  [the longest x2 15.3 us: spread(): held.append(lax.ppermute(part, 'tok', hop))]
  transfers between devices with their start and end apart: 10 -> 9, of which waited for: 6 -> 5; matrix products, arithmetic and copies ran while one was open for 27% -> 2% of each run, Pallas kernels for 0% -> 7%
where the time goes in v1:
time: 142 us
  waiting for transfers between devices  84.1 us (59%)
  Pallas kernels  30.3 us (21%)
  starting transfers between devices  18.2 us (13%)
  other arithmetic  4.94 us (3%)
  local copies, waits for them, and re-layouts  3.35 us (2%)
    all_to_all x3, waiting for transfers between devices, exchange(): return lax.all_to_all(x, 'cache', split_axis=0, concat_axis=0, tiled=True)  68 us
    pallas_call x1, Pallas kernels, attend_all(): pl.pallas_call(functools.partial(attend_kernel, spans, draft), grid=(reqs...  17.2 us
    ppermute x2, waiting for transfers between devices, spread(): held.append(lax.ppermute(part, 'tok', hop))  15.3 us
    all_to_all x3, starting transfers between devices, exchange(): return lax.all_to_all(x, 'cache', split_axis=0, concat_axis=0, tiled=True)  14.4 us
    pallas_call x3, Pallas kernels, take_rows(): pl.pallas_call(functools.partial(take_kernel, count), out_shape=jax.Shape...  9.52 us
    pallas_call x1, Pallas kernels, place_parts(): pl.pallas_call(functools.partial(place_kernel, spans, count), out_shape=j...  3.58 us
    ppermute x2, starting transfers between devices, spread(): held.append(lax.ppermute(part, 'tok', hop))  3.17 us
  transfers between devices with their start and end apart: 9, of which 5 were waited for; matrix products, arithmetic and copies ran while one was open for 2% of the time, Pallas kernels for 7%

profile of v1, /device:TPU:0, one launch (start us, length us, event | category | flops | bytes accessed | tf_op | source)
XLA Modules:
  0.0 141.6 jit_solution(13347775083132082529)
XLA Ops:
  0.6 0.8 select_reduce_fusion.3
  1.4 0.1 copy.20
  1.5 0.7 pad.12.clone
  2.2 0.7 broadcast_in_dim.73
  2.9 0.7 pad_add_fusion
  3.5 7.3 %all-to-all-start = ((s32[8,1,17]{2,1,0:T(1,128)}), s32[8,1,17]{2,1,0:T(1,128)S(1)}, u32[]{:S(2)}, u32[]{:S(2)}) async-start(s32[8,1,17]{2,1,0:T(1,128)} %bitcast.1), calls=%async_computation | async-start | bytes 8192 | tf_op jit(solution)/shard_map/all_to_all | solution.py:213
  10.8 6.4 %all-to-all-done = s32[8,1,17]{2,1,0:T(1,128)S(1)} async-done(((s32[8,1,17]{2,1,0:T(1,128)}), s32[8,1,17]{2,1,0:T(1,128)S(1)}, u32[]{:S(2)}, u32[]{:S(2)}) %all-to-all-start) | async-done | bytes 576 | tf_op jit(solution)/shard_map/all_to_all | solution.py:213
  17.2 0.6 slice_reduce_fusion.pick_ref
  17.9 3.3 %take_rows.3 = bf16[8,144,640]{2,1,0:T(8,128)(2,1)} custom-call(s32[8]{0:T(128)} %slice_reduce_fusion.pick_ref, s32[1]{0:T(128)} %bitcast.3.base_ref, bf16[8,576,640]{2,1,0:T(8,128)(2,1)} %bitcast.17), custom_call_target="tpu_custom_call" | custom-call | flops 2949120 | bytes 2949120 | tf_op jit(solution)/shard_map/take_rows/pallas_call | solution.py:43
  21.1 0.0 copy-start.6
  21.2 3.6 %all-to-all-start.1 = ((bf16[8,144,640]{2,1,0:T(8,128)(2,1)}), bf16[8,144,640]{2,1,0:T(8,128)(2,1)S(1)}, u32[]{:S(2)}, u32[]{:S(2)}) async-start(bf16[8,144,640]{2,1,0:T(8,128)(2,1)} %take_rows.3), calls=%async_computation.1 | async-start | bytes 2949120 | tf_op jit(solution)/shard_map/all_to_all | solution.py:213
  24.8 0.0 copy-done.6
  24.8 0.6 select_reduce_fusion.pick_ref
  25.4 3.5 %take_rows.4 = bf16[8,144,640]{2,1,0:T(8,128)(2,1)} custom-call(s32[8]{0:T(128)} %select_reduce_fusion.pick_ref, s32[1]{0:T(128)} %bitcast.3.base_ref, bf16[8,576,640]{2,1,0:T(8,128)(2,1)} %bitcast.18), custom_call_target="tpu_custom_call" | custom-call | flops 2949120 | bytes 2949120 | tf_op jit(solution)/shard_map/take_rows/pallas_call | solution.py:43
  28.9 0.0 copy-start.7
  28.9 29.7 %all-to-all-done.1.refs_3_ = bf16[8,144,640]{2,1,0:T(8,128)(2,1)S(1)} async-done(((bf16[8,144,640]{2,1,0:T(8,128)(2,1)}), bf16[8,144,640]{2,1,0:T(8,128)(2,1)S(1)}, u32[]{:S(2)}, u32[]{:S(2)}) %all-to-all-start.1) | async-done | bytes 1474592 | tf_op jit(solution)/shard_map/all_to_all | solution.py:213
  58.6 0.0 copy-start.1
  58.6 3.6 %all-to-all-start.2 = ((bf16[8,144,640]{2,1,0:T(8,128)(2,1)}), bf16[8,144,640]{2,1,0:T(8,128)(2,1)S(1)}, u32[]{:S(2)}, u32[]{:S(2)}) async-start(bf16[8,144,640]{2,1,0:T(8,128)(2,1)} %take_rows.4), calls=%async_computation.2 | async-start | bytes 2949120 | tf_op jit(solution)/shard_map/all_to_all | solution.py:213
  62.2 0.0 copy-start.4
  62.2 0.0 copy-start.5
  62.2 1.6 %collective-permute-start = (bf16[8,144,640]{2,1,0:T(8,128)(2,1)S(1)}, bf16[8,144,640]{2,1,0:T(8,128)(2,1)}, u32[]{:S(2)}, u32[]{:S(2)}) collective-permute-start(bf16[8,144,640]{2,1,0:T(8,128)(2,1)S(1)} %all-to-all-done.1.refs_3_), channel_id=1, source_target_pairs={{0,16},{8,24},{16,0},{24,8},{1,17},{9,25},{17,1},{25,9},{2,18},{10... | collective-permute-start | bytes 4423688 | tf_op jit(solution)/shard_map/ppermute | solution.py:248
  63.8 0.2 reduce-window.8
  64.0 0.0 copy-done.7
  64.0 0.6 select_reduce_fusion.1
  64.6 0.6 select_reduce_fusion.4.pick_ref
  65.2 31.9 %all-to-all-done.2.table_ref = bf16[8,144,640]{2,1,0:T(8,128)(2,1)S(1)} async-done(((bf16[8,144,640]{2,1,0:T(8,128)(2,1)}), bf16[8,144,640]{2,1,0:T(8,128)(2,1)S(1)}, u32[]{:S(2)}, u32[]{:S(2)}) %all-to-all-start.2) | async-done | bytes 1474592 | tf_op jit(solution)/shard_map/all_to_all | solution.py:213
  97.1 0.0 copy-start
  97.1 1.1 copy-done
  98.2 2.8 %take_rows.5.refs_0_ = bf16[4,144,640]{2,1,0:T(8,128)(2,1)} custom-call(s32[4]{0:T(128)} %select_reduce_fusion.4.pick_ref, s32[1]{0:T(128)} %constant.52.clone.1.base_ref, bf16[8,144,640]{2,1,0:T(8,128)(2,1)} %copy-done), custom_call_target="tpu_custom_call" | custom-call | flops 1474560 | bytes 1474560 | tf_op jit(solution)/shard_map/take_rows/pallas_call | solution.py:43
  101.0 1.6 %collective-permute-start.3 = (bf16[4,144,640]{2,1,0:T(8,128)(2,1)}, bf16[4,144,640]{2,1,0:T(8,128)(2,1)S(1)}, u32[]{:S(2)}, u32[]{:S(2)}) collective-permute-start(bf16[4,144,640]{2,1,0:T(8,128)(2,1)} %take_rows.5.refs_0_), channel_id=1, source_target_pairs={{0,16},{8,24},{16,0},{24,8},{1,17},{9,25},{17,1},{25,9},{2,18},{10... | collective-permute-start | bytes 2211848 | tf_op jit(solution)/shard_map/ppermute | solution.py:248
  102.5 0.0 copy-done.1
  102.5 0.0 collective-permute-start.1
  102.5 0.0 collective-permute-done.refs_4_
  102.6 0.5 collective-permute-start.2
  103.1 0.1 collective-permute-start.4
  103.1 15.3 %collective-permute-done.3.refs_1_ = bf16[4,144,640]{2,1,0:T(8,128)(2,1)S(1)} collective-permute-done((bf16[4,144,640]{2,1,0:T(8,128)(2,1)}, bf16[4,144,640]{2,1,0:T(8,128)(2,1)S(1)}, u32[]{:S(2)}, u32[]{:S(2)}) %collective-permute-start.3) | collective-permute-done | bytes 737312 | tf_op jit(solution)/shard_map/ppermute | solution.py:248
  118.4 0.0 copy-start.2
  118.4 0.0 collective-permute-start.5
  118.4 0.0 copy-done.4
  118.4 0.0 copy-done.5
  118.5 0.8 pad_add_fusion.1.starts_ref
  119.2 0.7 fusion.2.refs_2_
  120.0 0.0 collective-permute-done.4.refs_2_
  120.0 0.0 copy-start.3
  120.0 0.8 collective-permute-done.5.refs_3_
  120.8 0.0 copy-done.2
  120.8 0.1 copy-done.3
  120.8 3.6 %place_parts.1 = bf16[4,576,640]{2,1,0:T(8,128)(2,1)} custom-call(s32[4]{0:T(128)} %pad_add_fusion.1.starts_ref, bf16[4,144,640]{2,1,0:T(8,128)(2,1)} %take_rows.5.refs_0_, bf16[4,144,640]{2,1,0:T(8,128)(2,1)} %copy-done.2, bf16[4,144,640]{2,1,0:T(8,128)(2,1)} %copy-done.3, bf16[4,144,640]{2,1,0:T(8,128)(2,1)} %collective-permute-done.5.refs_3_), custom_call_target="tpu_custom_call" | custom-call | flops 5898240 | bytes 5898240 | tf_op jit(solution)/shard_map/place_parts/pallas_call | solution.py:82
  124.4 0.0 collective-permute-done.1.refs_5_
  124.4 0.0 collective-permute-done.2.refs_6_
  124.5 17.2 %attend_all.1 = (bf16[8,192,512]{2,1,0:T(8,128)(2,1)}, bf16[8,192,512]{2,1,0:T(8,128)(2,1)}) custom-call(s32[8]{0:T(128)} %owner_ref.1, s32[8]{0:T(128)} %get-tuple-element.8.length_ref, s32[8]{0:T(128)} %accept_ref.1, s32[4]{0:T(128)} %pad_add_fusion.1.starts_ref, bf16[8,192,576]{2,1,0:T(8,128)(2,1)} %bitcast.23, bf16[8,192,576]{2,1,0:T(8,128)(2,1)} %bitcast.24, ...), custom_call_target="tpu_custom_call" | custom-call | flops 4278190080 | bytes 11796480 | tf_op jit(solution)/shard_map/attend_all/pallas_call | solution.py:169
  (4 shorter events, 0.0 us)
Async XLA Ops:
  3.5 13.7 %all-to-all-start = ((s32[8,1,17]{2,1,0:T(1,128)}), s32[8,1,17]{2,1,0:T(1,128)S(1)}, u32[]{:S(2)}, u32[]{:S(2)}) async-start(s32[8,1,17]{2,1,0:T(1,128)} %bitcast.1), calls=%async_computation | async-start | bytes 8192 | tf_op jit(solution)/shard_map/all_to_all | solution.py:213
  21.1 3.6 %copy-start.6 = (s32[8]{0:T(128)S(1)}, s32[8]{0:T(128)}, u32[]{:S(2)}) copy-start(s32[8]{0:T(128)} %param.16) | copy-start | bytes 100
  21.2 37.5 %all-to-all-start.1 = ((bf16[8,144,640]{2,1,0:T(8,128)(2,1)}), bf16[8,144,640]{2,1,0:T(8,128)(2,1)S(1)}, u32[]{:S(2)}, u32[]{:S(2)}) async-start(bf16[8,144,640]{2,1,0:T(8,128)(2,1)} %take_rows.3), calls=%async_computation.1 | async-start | bytes 2949120 | tf_op jit(solution)/shard_map/all_to_all | solution.py:213
  28.9 35.1 %copy-start.7 = (s32[8]{0:T(128)S(1)}, s32[8]{0:T(128)}, u32[]{:S(2)}) copy-start(s32[8]{0:T(128)} %owner_ref.1) | copy-start | bytes 100
  58.6 43.9 %copy-start.1 = (bf16[8,144,640]{2,1,0:T(8,128)(2,1)}, bf16[8,144,640]{2,1,0:T(8,128)(2,1)S(1)}, u32[]{:S(2)}) copy-start(bf16[8,144,640]{2,1,0:T(8,128)(2,1)S(1)} %all-to-all-done.1.refs_3_) | copy-start | bytes 4423684
  58.6 38.5 %all-to-all-start.2 = ((bf16[8,144,640]{2,1,0:T(8,128)(2,1)}), bf16[8,144,640]{2,1,0:T(8,128)(2,1)S(1)}, u32[]{:S(2)}, u32[]{:S(2)}) async-start(bf16[8,144,640]{2,1,0:T(8,128)(2,1)} %take_rows.4), calls=%async_computation.2 | async-start | bytes 2949120 | tf_op jit(solution)/shard_map/all_to_all | solution.py:213
  62.2 56.2 %copy-start.4 = (bf16[8,6,576]{2,0,1:T(8,128)(2,1)S(1)}, bf16[8,6,576]{2,0,1:T(8,128)(2,1)}, u32[]{:S(2)}) copy-start(bf16[8,6,576]{2,0,1:T(8,128)(2,1)} %param.12) | copy-start | bytes 165892
  62.2 56.2 %copy-start.5 = (bf16[8,6,576]{2,0,1:T(8,128)(2,1)S(1)}, bf16[8,6,576]{2,0,1:T(8,128)(2,1)}, u32[]{:S(2)}) copy-start(bf16[8,6,576]{2,0,1:T(8,128)(2,1)} %param.10) | copy-start | bytes 165892
  62.2 40.3 %collective-permute-start = (bf16[8,144,640]{2,1,0:T(8,128)(2,1)S(1)}, bf16[8,144,640]{2,1,0:T(8,128)(2,1)}, u32[]{:S(2)}, u32[]{:S(2)}) collective-permute-start(bf16[8,144,640]{2,1,0:T(8,128)(2,1)S(1)} %all-to-all-done.1.refs_3_), channel_id=1, source_target_pairs={{0,16},{8,24},{16,0},{24,8},{1,17},{9,25},{17,1},{25,9},{2,18},{10... | collective-permute-start | bytes 4423688 | tf_op jit(solution)/shard_map/ppermute | solution.py:248
  97.1 1.1 copy-start
  101.0 17.5 %collective-permute-start.3 = (bf16[4,144,640]{2,1,0:T(8,128)(2,1)}, bf16[4,144,640]{2,1,0:T(8,128)(2,1)S(1)}, u32[]{:S(2)}, u32[]{:S(2)}) collective-permute-start(bf16[4,144,640]{2,1,0:T(8,128)(2,1)} %take_rows.5.refs_0_), channel_id=1, source_target_pairs={{0,16},{8,24},{16,0},{24,8},{1,17},{9,25},{17,1},{25,9},{2,18},{10... | collective-permute-start | bytes 2211848 | tf_op jit(solution)/shard_map/ppermute | solution.py:248
  102.5 21.9 %collective-permute-start.1 = (bf16[8,144,640]{2,1,0:T(8,128)(2,1)S(1)}, bf16[8,144,640]{2,1,0:T(8,128)(2,1)}, u32[]{:S(2)}, u32[]{:S(2)}) collective-permute-start(bf16[8,144,640]{2,1,0:T(8,128)(2,1)S(1)} %all-to-all-done.1.refs_3_), channel_id=1, source_target_pairs={{0,8},{8,0},{16,24},{24,16},{1,9},{9,1},{17,25},{25,17},{2,10},{10... | collective-permute-start | bytes 4423688 | tf_op jit(solution)/shard_map/ppermute | solution.py:250
  102.6 21.9 %collective-permute-start.2 = (bf16[8,144,640]{2,1,0:T(8,128)(2,1)}, bf16[8,144,640]{2,1,0:T(8,128)(2,1)}, u32[]{:S(2)}, u32[]{:S(2)}) collective-permute-start(bf16[8,144,640]{2,1,0:T(8,128)(2,1)} %collective-permute-done.refs_4_), channel_id=1, source_target_pairs={{0,8},{8,0},{16,24},{24,16},{1,9},{9,1},{17,25},{25,17},{2,10},{10... | collective-permute-start | bytes 4423688 | tf_op jit(solution)/shard_map/ppermute | solution.py:250
  103.1 16.9 %collective-permute-start.4 = (bf16[4,144,640]{2,1,0:T(8,128)(2,1)}, bf16[4,144,640]{2,1,0:T(8,128)(2,1)S(1)}, u32[]{:S(2)}, u32[]{:S(2)}) collective-permute-start(bf16[4,144,640]{2,1,0:T(8,128)(2,1)} %take_rows.5.refs_0_), channel_id=1, source_target_pairs={{0,8},{8,0},{16,24},{24,16},{1,9},{9,1},{17,25},{25,17},{2,10},{10... | collective-permute-start | bytes 2211848 | tf_op jit(solution)/shard_map/ppermute | solution.py:250
  118.4 2.4 %copy-start.2 = (bf16[4,144,640]{2,1,0:T(8,128)(2,1)}, bf16[4,144,640]{2,1,0:T(8,128)(2,1)S(1)}, u32[]{:S(2)}) copy-start(bf16[4,144,640]{2,1,0:T(8,128)(2,1)S(1)} %collective-permute-done.3.refs_1_) | copy-start | bytes 2211844
  118.4 2.3 %collective-permute-start.5 = (bf16[4,144,640]{2,1,0:T(8,128)(2,1)S(1)}, bf16[4,144,640]{2,1,0:T(8,128)(2,1)}, u32[]{:S(2)}, u32[]{:S(2)}) collective-permute-start(bf16[4,144,640]{2,1,0:T(8,128)(2,1)S(1)} %collective-permute-done.3.refs_1_), channel_id=1, source_target_pairs={{0,8},{8,0},{16,24},{24,16},{1,9},{9,1},{17,25},{25,17},{2,10},{10... | collective-permute-start | bytes 2211848 | tf_op jit(solution)/shard_map/ppermute | solution.py:250
  120.0 0.9 copy-start.3

commit v2 on v1

v2 whole, which is shorter than its diff:
```python
import functools

import jax
import jax.numpy as jnp
from jax import lax
from jax.experimental import pallas as pl
from jax.experimental.pallas import tpu as pltpu
from jax.sharding import PartitionSpec as P


LAT = 512
CORES = 2
ROWS = 16

score_factor = 192.0 ** (-0.5)
log2_e = 1.4426950408889634
ANY = pl.BlockSpec(memory_space=pl.ANY)
SMEM = pl.BlockSpec(memory_space=pltpu.SMEM)
VMEM = pl.BlockSpec(memory_space=pltpu.VMEM)


def round_up(value, step):
    return -(-value // step) * step


def tell_kernel(first_ref, length_ref, move_ref, out_ref):
    reqs = first_ref.shape[0]
    lane = lax.broadcasted_iota(jnp.int32, out_ref.shape, 1)
    row = jnp.zeros(out_ref.shape, jnp.int32)
    for t, ref in enumerate((first_ref, length_ref, move_ref)):
        for j in range(reqs):
            row = jnp.where(lane == t * reqs + j, ref[j], row)
    out_ref[...] = row


def tell(first_owner, cached_len, new_owner, peers):
    return pl.pallas_call(
        tell_kernel,
        out_shape=jax.ShapeDtypeStruct((peers, 3 * first_owner.shape[0]), jnp.int32),
        in_specs=[SMEM] * 3,
        out_specs=VMEM,
        name="tell",
    )(first_owner, cached_len, new_owner)


def peer_of(me, half, s, to):
    side, place = me // half, me % half
    if s < half:
        return side * half + s
    shift = s - half if to else 2 * half - s
    return (1 - side) * half + lax.rem(place + shift, half)


def take_kernel(plan, half, moves, meta_ref, slots_ref, table_ref, *refs):
    outs, sems = refs[: len(plan)], refs[len(plan)]
    me = meta_ref[0]
    copies = []
    for out_ref, (first, part) in zip(outs, plan):
        base = pl.multiple_of(meta_ref[part], ROWS)
        for d in range(out_ref.shape[0]):
            peer = peer_of(me, half, first + d, True)
            slot = jnp.int32(0)
            for j in range(2 * half):
                if moves:
                    hit = (slots_ref[j] == peer) & (peer != me)
                else:
                    hit = slots_ref[peer, j] == me
                slot = jnp.where(hit, j, slot)
            copies.append(
                pltpu.make_async_copy(
                    table_ref.at[slot, pl.ds(base, out_ref.shape[1])],
                    out_ref.at[d],
                    sems.at[first + d],
                )
            )
    for copy in copies:
        copy.start()
    for copy in copies:
        copy.wait()


def take_rows(table, meta, slots, moves, plan, shapes):
    lanes = table.shape[2]
    count = sum(shape[0] for shape in shapes)
    size = sum(n * rows for n, rows in shapes) * lanes * table.dtype.itemsize
    return pl.pallas_call(
        functools.partial(take_kernel, plan, count // 2, moves),
        out_shape=[jax.ShapeDtypeStruct(shape + (lanes,), table.dtype) for shape in shapes],
        in_specs=[SMEM, SMEM, ANY],
        out_specs=[VMEM] * len(shapes),
        scratch_shapes=[pltpu.SemaphoreType.DMA((count,))],
        cost_estimate=pl.CostEstimate(flops=2 * size, bytes_accessed=2 * size, transcendentals=0),
        name="take_rows",
    )(meta, slots, table)


def place_kernel(groups, kept, half, meta_ref, heard_ref, move_ref, *refs):
    count = len(groups)
    reqs = move_ref.shape[0]
    me = meta_ref[0]
    order, leaves = [], []
    rank = jnp.int32(0)
    for j in range(reqs):
        leaves.append(move_ref[j] != me)
        order.append(rank)
        rank = rank + leaves[-1].astype(jnp.int32)
    dests = {}
    for source in sorted({source + i for source, i in spans_of(groups, refs)}):
        peer = peer_of(me, half, source, False)
        dest = jnp.int32(-1)
        for j in range(reqs):
            hit = leaves[j] & (heard_ref[peer, 2 * reqs + j] == me)
            dest = jnp.where(hit, order[j], dest)
        dests[source] = dest
    parts, out_ref, bufs = refs[:count], refs[count + kept], refs[count + kept + 1 : -2]
    in_sems, out_sems = refs[-2:]
    steps = []
    for p, (source, origin) in enumerate(groups):
        base = pl.multiple_of(meta_ref[origin], ROWS)
        for i in range(parts[p].shape[0]):
            dest = dests[source + i]
            load = pltpu.make_async_copy(parts[p].at[i], bufs[p].at[i], in_sems.at[p, i])
            store = pltpu.make_async_copy(
                bufs[p].at[i],
                out_ref.at[jnp.maximum(dest, 0), pl.ds(base, parts[p].shape[1])],
                out_sems.at[p, i],
            )
            steps.append((dest >= 0, load, store))
    for used, load, store in steps:
        pl.when(used)(load.start)
    for used, load, store in steps:

        @pl.when(used)
        def _(load=load, store=store):
            load.wait()
            store.start()

    for used, load, store in steps:
        pl.when(used)(store.wait)


def spans_of(groups, parts):
    return [(source, i) for (source, _), part in zip(groups, parts) for i in range(part.shape[0])]


def place_parts(parts, groups, meta, heard, moves, shape, out=None):
    dtype = parts[0].dtype
    size = shape[0] * shape[1] * shape[2] * dtype.itemsize
    kept = [] if out is None else [out]
    most = max(part.shape[0] for part in parts)
    return pl.pallas_call(
        functools.partial(place_kernel, groups, len(kept), heard.shape[0] // 2),
        out_shape=jax.ShapeDtypeStruct(shape, dtype),
        in_specs=[SMEM] * 3 + [ANY] * (len(parts) + len(kept)),
        out_specs=ANY,
        input_output_aliases={3 + len(parts): 0} if kept else {},
        scratch_shapes=[pltpu.VMEM(part.shape, dtype) for part in parts]
        + [pltpu.SemaphoreType.DMA((len(parts), most))] * 2,
        cost_estimate=pl.CostEstimate(flops=size, bytes_accessed=size, transcendentals=0),
        name="place_parts",
    )(meta, heard, moves, *parts, *kept)


def attend(queries, keys_t, length, extra, extra_mask):
    scale = score_factor * log2_e
    near = jnp.dot(queries, keys_t, preferred_element_type=jnp.float32) * scale
    places = lax.broadcasted_iota(jnp.int32, (1, keys_t.shape[1]), 1)
    near = jnp.where(places < length, near, -jnp.inf)
    own = (
        lax.dot_general(
            queries, extra, (((1,), (1,)), ((), ())), preferred_element_type=jnp.float32
        )
        * scale
    )
    own = jnp.where(extra_mask, own, -jnp.inf)
    row_max = jnp.maximum(
        jnp.max(near, axis=1, keepdims=True), jnp.max(own, axis=1, keepdims=True)
    )
    near_weight = jnp.exp2(near - row_max)
    own_weight = jnp.exp2(own - row_max)
    total = jnp.sum(near_weight, axis=1, keepdims=True) + jnp.sum(
        own_weight, axis=1, keepdims=True
    )
    mixture = lax.dot_general(
        near_weight.astype(jnp.bfloat16),
        keys_t[:LAT],
        (((1,), (1,)), ((), ())),
        preferred_element_type=jnp.float32,
    )
    mixture = mixture + jnp.dot(
        own_weight.astype(jnp.bfloat16), extra[:, :LAT], preferred_element_type=jnp.float32
    )
    return (mixture * (1.0 / total)).astype(jnp.bfloat16)


def attend_kernel(groups, kept, half, meta_ref, heard_ref, first_ref, accept_ref, row_ref, *refs):
    parts = refs[: len(groups)]
    q1_ref, q2_ref, k1_ref, k2_ref = refs[len(groups) : len(groups) + 4]
    o1_ref, o2_ref, held, sems = refs[len(groups) + 4 + kept :]
    step = pl.program_id(0)
    me = meta_ref[0]
    base_slot = groups[0][0]

    @pl.when(step == 0)
    def _():
        used = {}
        for (request, origin), part in zip(groups, parts):
            base = pl.multiple_of(meta_ref[origin], ROWS)
            for i in range(part.shape[0]):
                slot = request + i - base_slot
                sem = used[slot] = used.get(slot, -1) + 1
                pltpu.make_async_copy(
                    part.at[i], held.at[slot, pl.ds(base, part.shape[1])], sems.at[slot, sem]
                ).start()

    request = row_ref[step]
    peer = first_ref[request]
    side = (peer // half == me // half).astype(jnp.int32)
    far = half + lax.rem(me + 2 * half - peer, half)
    slot = jnp.where(side == 1, lax.rem(peer, half), far) - base_slot
    for p in range(sems.shape[1]):
        rows = parts[0].shape[1]
        pltpu.make_async_copy(
            parts[0].at[0], held.at[slot, pl.ds(0, rows)], sems.at[slot, p]
        ).wait()

    rows = q1_ref.shape[1]
    reqs = first_ref.shape[0]
    draft = k1_ref.shape[0] // reqs
    heads = rows // draft
    keys = jnp.concatenate([k1_ref[...], k2_ref[...]], axis=0)
    row = lax.broadcasted_iota(jnp.int32, (rows, 1), 0)
    col = lax.broadcasted_iota(jnp.int32, (1, keys.shape[0]), 1)
    key = lax.div(col, reqs)
    own = lax.rem(col, reqs) == request
    first = own & (key < draft)
    causal = row >= lax.rem(key, draft) * heads
    taken = first & (key < accept_ref[request])
    keys_t = held[slot]
    length = heard_ref[peer, reqs + request]
    o1_ref[0] = attend(q1_ref[0], keys_t, length, keys, first & causal)
    o2_ref[0] = attend(
        q2_ref[0], keys_t, length, keys, taken | (own & (key >= draft) & causal)
    )


def attend_some(q1, q2, k1, k2, parts, groups, meta, heard, first, accepted, rows_of, outs=()):
    reqs, rows, width = q1.shape
    count = rows_of.shape[0]
    positions = parts[0].shape[2]
    each = sum(part.shape[0] for part in parts) // count
    block = lambda lanes: pl.BlockSpec((1, rows, lanes), lambda r, *refs: (refs[4][r], 0, 0))
    whole = pl.BlockSpec(k1.shape, lambda r, *_: (0, 0))
    out = jax.ShapeDtypeStruct((reqs, rows, LAT), jnp.bfloat16)
    flops = 2 * 2 * count * rows * positions * (width + LAT)
    start = 5 + len(parts) + 4
    return pl.pallas_call(
        functools.partial(attend_kernel, groups, len(outs), heard.shape[0] // 2),
        grid_spec=pltpu.PrefetchScalarGridSpec(
            num_scalar_prefetch=5,
            grid=(count,),
            in_specs=[ANY] * len(parts)
            + [block(width), block(width), whole, whole]
            + [ANY] * len(outs),
            out_specs=[block(LAT), block(LAT)],
            scratch_shapes=[
                pltpu.VMEM((count, width, positions), jnp.bfloat16),
                pltpu.SemaphoreType.DMA((count, each)),
            ],
        ),
        out_shape=(out, out),
        input_output_aliases={start + i: i for i in range(len(outs))},
        cost_estimate=pl.CostEstimate(
            flops=flops, bytes_accessed=count * width * positions * 4, transcendentals=0
        ),
        compiler_params=pltpu.CompilerParams(dimension_semantics=("arbitrary",)),
        name="attend_some",
    )(meta, heard, first, accepted, rows_of, *parts, q1, q2, k1, k2, *outs)


def program(
    queries_one,
    keys_one,
    queries_two,
    keys_two,
    latent_cache,
    cached_len,
    first_owner,
    new_owner,
    accepted,
):
    peers = lax.axis_size("cache")
    me = lax.axis_index("cache")
    groups = lax.axis_size("tok")
    group = lax.axis_index("tok")
    chips = groups // CORES
    reqs, draft, heads, width = queries_one.shape
    half = peers // 2
    halves = [[h * half + i for i in range(half)] for h in range(2)]

    def near_exchange(x):
        return lax.all_to_all(
            x, "cache", split_axis=0, concat_axis=0, tiled=True, axis_index_groups=halves
        )

    def far_shift(x, s):
        hop = [
            (h * half + i, (1 - h) * half + (i + s) % half) for h in range(2) for i in range(half)
        ]
        return lax.ppermute(x, "cache", hop)

    told = tell(first_owner, cached_len, new_owner, peers)
    heard = lax.all_to_all(told, "cache", split_axis=0, concat_axis=0, tiled=True)

    cache_t = jnp.swapaxes(latent_cache, 1, 2)
    share = round_up(-(-width // groups), ROWS)
    start_of = lambda t: jnp.minimum(t * share, width - share).astype(jnp.int32)
    chip, core = group // CORES, group % CORES
    origins = [group] + [(chip + chips - s) % chips * CORES + core for s in range(1, chips)]
    origins += [t + 1 - 2 * core for t in origins]
    wide = round_up(-(-width // CORES), ROWS)
    wide_of = lambda k: jnp.minimum(k * wide, width - wide).astype(jnp.int32)
    meta = jnp.stack(
        [me.astype(jnp.int32)]
        + [start_of(t) for t in origins]
        + [wide_of(core), wide_of(1 - core)]
    )
    swap = [(t, t + 1 - 2 * (t % CORES)) for t in range(groups)]

    def spread(part):
        held = [part]
        for s in range(1, chips):
            hop = [
                (c * CORES + k, (c + s) % chips * CORES + k)
                for c in range(chips)
                for k in range(CORES)
            ]
            held.append(lax.ppermute(part, "tok", hop))
        for x in held[:]:
            held.append(lax.ppermute(x, "tok", swap))
        return held

    plan = [(0, groups + 1)] + [(half + s, 1) for s in range(half)]
    sent = take_rows(
        cache_t, meta, new_owner, True, plan, [(half, wide)] + [(1, share)] * half
    )
    move_far = []
    for s in range(half):
        move_far.append(far_shift(sent[1 + s], s))
    move_near = near_exchange(sent[0])

    plan = [(0, 1)] + [(half + s, 1) for s in range(half)]
    sent = take_rows(cache_t, meta, heard, False, plan, [(half, share)] + [(1, share)] * half)
    draft_far = []
    for s in range(half):
        draft_far.append(far_shift(sent[1 + s], s))
    draft_near = near_exchange(sent[0])

    flat = (reqs, draft * heads, width)
    keys = (draft * reqs, width)
    operands = (
        queries_one.reshape(flat),
        queries_two.reshape(flat),
        jnp.swapaxes(keys_one, 0, 1).reshape(keys),
        jnp.swapaxes(keys_two, 0, 1).reshape(keys),
    )
    scalars = (meta, heard, first_owner, accepted)

    parts = spread(draft_near)
    where = [(0, 1 + k) for k in range(groups)]
    for s in range(half):
        parts += spread(draft_far[s])
        where += [(half + s, 1 + k) for k in range(groups)]
    rows_of = jnp.arange(reqs, dtype=jnp.int32)
    outs = attend_some(*operands, parts, where, *scalars, rows_of)

    tables = (meta, heard, new_owner)
    shape = (peers // 2, width, cache_t.shape[2])
    parts = [move_near, lax.ppermute(move_near, "tok", swap)]
    where = [(0, groups + 1), (0, groups + 2)]
    arrived = place_parts(parts, where, *tables, shape)
    parts, where = [], []
    for s in range(half):
        parts += spread(move_far[s])
        where += [(half + s, 1 + k) for k in range(groups)]
    arrived = place_parts(parts, where, *tables, shape, arrived)

    shape = (reqs, draft, heads, LAT)
    return outs[0].reshape(shape), outs[1].reshape(shape), jnp.swapaxes(arrived, 1, 2)


def solution(mesh):
    placed = (
        P("cache", None, "tok", None),
        P("cache", None, None),
        P("cache", None, "tok", None),
        P("cache", None, None),
        P("cache", None, None),
        P("cache"),
        P("cache"),
        P("cache"),
        P("cache"),
    )
    return jax.shard_map(
        program,
        mesh=mesh,
        in_specs=placed,
        out_specs=(
            P("cache", None, "tok", None),
            P("cache", None, "tok", None),
            P("cache", None, None),
        ),
        check_vma=False,
    )
```

time: 142 us -> 177 us (1.25)
  starting transfers between devices: 18.2 us -> 53.2 us
  other arithmetic: 4.94 us -> 0 us
  Pallas kernels: 30.3 us -> 34 us
    all_to_all x3, waiting for transfers between devices: 68 us -> 11.3 us  [the longest x1 5.85 us: program(): lax.all_to_all(told, 'cache', split_axis=0, concat_axis=0, tiled=True)]
    ppermute x4 -> x27, waiting for transfers between devices: 0.81 us -> 44.5 us  [the longest x8 42.6 us: far_shift(): return lax.ppermute(x, 'cache', hop)]
    ppermute x4 -> x27, starting transfers between devices: 0.58 us -> 24.5 us  [the longest x8 21.6 us: far_shift(): return lax.ppermute(x, 'cache', hop)]
    ppermute x2 -> x9, waiting for transfers between devices: 15.3 us -> 29.6 us  [spread(): held.append(lax.ppermute(part, 'tok', hop))]
    ppermute x2 -> x9, starting transfers between devices: 3.17 us -> 13.6 us  [spread(): held.append(lax.ppermute(part, 'tok', hop))]
    pallas_call x5 -> x6, Pallas kernels: 30.3 us -> 34 us  [the longest x1 19.5 us: attend_some(): pl.pallas_call(functools.partial(attend_kernel, groups, len(outs), heard....]
    reduce_sum x4 -> x0, other arithmetic: 2.6 us -> none  [pick(): return jnp.sum(jnp.where(hits, table, 0), axis=axis, dtype=jnp.int32)]
  transfers between devices with their start and end apart: 9 -> 39, of which waited for: 5 -> 17; matrix products, arithmetic and copies ran while one was open for 2% -> 1% of each run, Pallas kernels for 7% -> 15%
where the time goes in v2:
time: 177 us; the launch traced here: 176 us
  waiting for transfers between devices  85.5 us (48%)
  starting transfers between devices  53.2 us (30%)
  Pallas kernels  34 us (19%)
  local copies, waits for them, and re-layouts  2.25 us (1%)
    ppermute x8, waiting for transfers between devices, far_shift(): return lax.ppermute(x, 'cache', hop)  42.6 us
    ppermute x9, waiting for transfers between devices, spread(): held.append(lax.ppermute(part, 'tok', hop))  29.6 us
    ppermute x8, starting transfers between devices, far_shift(): return lax.ppermute(x, 'cache', hop)  21.6 us
    pallas_call x1, Pallas kernels, attend_some(): pl.pallas_call(functools.partial(attend_kernel, groups, len(outs), heard....  19.5 us
    ppermute x9, starting transfers between devices, spread(): held.append(lax.ppermute(part, 'tok', hop))  13.6 us
    all_to_all x2, starting transfers between devices, near_exchange(): lax.all_to_all(x, 'cache', split_axis=0, concat_axis=0, tiled=True, axis_...  7.75 us
    all_to_all x1, starting transfers between devices, program(): lax.all_to_all(told, 'cache', split_axis=0, concat_axis=0, tiled=True)  7.28 us
    pallas_call x2, Pallas kernels, take_rows(): pl.pallas_call(functools.partial(take_kernel, plan, count // 2, moves), o...  7.01 us
  transfers between devices with their start and end apart: 39, of which 17 were waited for; matrix products, arithmetic and copies ran while one was open for 1% of the time, Pallas kernels for 15%

profile of v2, /device:TPU:0, one launch (start us, length us, event | category | flops | bytes accessed | tf_op | source)
XLA Modules:
  0.0 176.0 jit_solution(17022083195198424018)
XLA Ops:
  0.6 1.3 tell.1
  1.9 7.3 %all-to-all-start = ((s32[8,1,24]{2,1,0:T(1,128)}), s32[8,1,24]{2,1,0:T(1,128)S(1)}, u32[]{:S(2)}, u32[]{:S(2)}) async-start(s32[8,1,24]{2,1,0:T(1,128)} %bitcast.30), calls=%async_computation | async-start | bytes 8192 | tf_op jit(solution)/shard_map/all_to_all | solution.py:313
  9.2 0.6 stack.31.meta_ref
  9.8 5.8 %all-to-all-done = s32[8,1,24]{2,1,0:T(1,128)S(1)} async-done(((s32[8,1,24]{2,1,0:T(1,128)}), s32[8,1,24]{2,1,0:T(1,128)S(1)}, u32[]{:S(2)}, u32[]{:S(2)}) %all-to-all-start) | async-done | bytes 800 | tf_op jit(solution)/shard_map/all_to_all | solution.py:313
  15.6 0.6 copy-done.8
  16.2 3.4 %take_rows.2 = (bf16[4,144,640]{2,1,0:T(8,128)(2,1)}, bf16[1,144,640]{2,1,0:T(8,128)(2,1)}, bf16[1,144,640]{2,1,0:T(8,128)(2,1)}, bf16[1,144,640]{2,1,0:T(8,128)(2,1)}, bf16[1,144,640]{2,1,0:T(8,128)(2,1)}) custom-call(s32[7]{0:T(128)} %stack.31.meta_ref, s32[8,24]{1,0:T(8,128)} %bitcast.26, bf16[8,576,640]{2,1,0:T(8,128)(2,1)} %bitcast.23), custom_call_target="tpu_custom_call" | custom-call | flops 2949120 | bytes 2949120 | tf_op jit(solution)/shard_map/take_rows/pallas_call | solution.py:86
  19.6 4.2 %all-to-all-start.1 = ((bf16[4,144,640]{2,1,0:T(8,128)(2,1)}), bf16[4,144,640]{2,1,0:T(8,128)(2,1)}, u32[]{:S(2)}, u32[]{:S(2)}) async-start(bf16[4,144,640]{2,1,0:T(8,128)(2,1)} %get-tuple-element.15), calls=%async_computation.1 | async-start | bytes 1474560 | tf_op jit(solution)/shard_map/all_to_all | solution.py:302
  23.8 3.6 %take_rows.3 = (bf16[4,288,640]{2,1,0:T(8,128)(2,1)}, bf16[1,144,640]{2,1,0:T(8,128)(2,1)}, bf16[1,144,640]{2,1,0:T(8,128)(2,1)}, bf16[1,144,640]{2,1,0:T(8,128)(2,1)}, bf16[1,144,640]{2,1,0:T(8,128)(2,1)}) custom-call(s32[7]{0:T(128)} %stack.31.meta_ref, s32[8]{0:T(128)} %move_ref.5, bf16[8,576,640]{2,1,0:T(8,128)(2,1)} %bitcast.24), custom_call_target="tpu_custom_call" | custom-call | flops 4423680 | bytes 4423680 | tf_op jit(solution)/shard_map/take_rows/pallas_call | solution.py:86
  27.5 0.0 copy-start.23
  27.5 5.5 %all-to-all-done.1.refs_0_ = bf16[4,144,640]{2,1,0:T(8,128)(2,1)} async-done(((bf16[4,144,640]{2,1,0:T(8,128)(2,1)}), bf16[4,144,640]{2,1,0:T(8,128)(2,1)}, u32[]{:S(2)}, u32[]{:S(2)}) %all-to-all-start.1) | async-done | bytes 737312 | tf_op jit(solution)/shard_map/all_to_all | solution.py:302
  33.0 3.6 %all-to-all-start.2 = ((bf16[4,288,640]{2,1,0:T(8,128)(2,1)}), bf16[4,288,640]{2,1,0:T(8,128)(2,1)S(1)}, u32[]{:S(2)}, u32[]{:S(2)}) async-start(bf16[4,288,640]{2,1,0:T(8,128)(2,1)} %get-tuple-element.26), calls=%async_computation.2 | async-start | bytes 2949120 | tf_op jit(solution)/shard_map/all_to_all | solution.py:302
  36.6 0.6 collective-permute-start.19
  37.2 3.7 %collective-permute-start.23 = (bf16[1,144,640]{2,1,0:T(8,128)(2,1)S(1)}, bf16[1,144,640]{2,1,0:T(8,128)(2,1)S(1)}, u32[]{:S(2)}, u32[]{:S(2)}) collective-permute-start(bf16[1,144,640]{2,1,0:T(8,128)(2,1)S(1)} %copy-done.30), channel_id=1, source_target_pairs={{0,5},{1,6},{2,7},{3,4},{4,1},{5,2},{6,3},{7,0},{8,13},{9,14},{10,... | collective-permute-start | bytes 552968 | tf_op jit(solution)/shard_map/ppermute | solution.py:310
  40.9 1.5 collective-permute-start.27
  42.4 3.3 %collective-permute-start.31 = (bf16[1,144,640]{2,1,0:T(8,128)(2,1)S(1)}, bf16[1,144,640]{2,1,0:T(8,128)(2,1)S(1)}, u32[]{:S(2)}, u32[]{:S(2)}) collective-permute-start(bf16[1,144,640]{2,1,0:T(8,128)(2,1)S(1)} %copy-done.28), channel_id=1, source_target_pairs={{0,7},{1,4},{2,5},{3,6},{4,3},{5,0},{6,1},{7,2},{8,15},{9,12},{10,... | collective-permute-start | bytes 552968 | tf_op jit(solution)/shard_map/ppermute | solution.py:310
  45.7 12.0 %collective-permute-done.19.refs_0_ = bf16[1,144,640]{2,1,0:T(8,128)(2,1)S(1)} collective-permute-done((bf16[1,144,640]{2,1,0:T(8,128)(2,1)S(1)}, bf16[1,144,640]{2,1,0:T(8,128)(2,1)S(1)}, u32[]{:S(2)}, u32[]{:S(2)}) %collective-permute-start.19) | collective-permute-done | bytes 184352 | tf_op jit(solution)/shard_map/ppermute | solution.py:310
  57.7 6.3 %collective-permute-start.7 = (bf16[1,144,640]{2,1,0:T(8,128)(2,1)S(1)}, bf16[1,144,640]{2,1,0:T(8,128)(2,1)S(1)}, u32[]{:S(2)}, u32[]{:S(2)}) collective-permute-start(bf16[1,144,640]{2,1,0:T(8,128)(2,1)S(1)} %copy-done.21), channel_id=1, source_target_pairs={{0,5},{1,6},{2,7},{3,4},{4,1},{5,2},{6,3},{7,0},{8,13},{9,14},{10,... | collective-permute-start | bytes 552968 | tf_op jit(solution)/shard_map/ppermute | solution.py:310
  64.0 2.5 %collective-permute-done.23.refs_4_ = bf16[1,144,640]{2,1,0:T(8,128)(2,1)S(1)} collective-permute-done((bf16[1,144,640]{2,1,0:T(8,128)(2,1)S(1)}, bf16[1,144,640]{2,1,0:T(8,128)(2,1)S(1)}, u32[]{:S(2)}, u32[]{:S(2)}) %collective-permute-start.23) | collective-permute-done | bytes 184352 | tf_op jit(solution)/shard_map/ppermute | solution.py:310
  66.5 2.3 %collective-permute-start.11 = (bf16[1,144,640]{2,1,0:T(8,128)(2,1)S(1)}, bf16[1,144,640]{2,1,0:T(8,128)(2,1)}, u32[]{:S(2)}, u32[]{:S(2)}) collective-permute-start(bf16[1,144,640]{2,1,0:T(8,128)(2,1)S(1)} %copy-done.19), channel_id=1, source_target_pairs={{0,6},{1,7},{2,4},{3,5},{4,2},{5,3},{6,0},{7,1},{8,14},{9,15},{10,... | collective-permute-start | bytes 552968 | tf_op jit(solution)/shard_map/ppermute | solution.py:310
  68.8 0.0 collective-permute-done.27.refs_8_
  68.8 3.9 %collective-permute-start.15 = (bf16[1,144,640]{2,1,0:T(8,128)(2,1)}, bf16[1,144,640]{2,1,0:T(8,128)(2,1)}, u32[]{:S(2)}, u32[]{:S(2)}) collective-permute-start(bf16[1,144,640]{2,1,0:T(8,128)(2,1)} %get-tuple-element.19), channel_id=1, source_target_pairs={{0,7},{1,4},{2,5},{3,6},{4,3},{5,0},{6,1},{7,2},{8,15},{9,12},{10,... | collective-permute-start | bytes 552968 | tf_op jit(solution)/shard_map/ppermute | solution.py:310
  72.8 17.1 %collective-permute-done.31.refs_12_ = bf16[1,144,640]{2,1,0:T(8,128)(2,1)S(1)} collective-permute-done((bf16[1,144,640]{2,1,0:T(8,128)(2,1)S(1)}, bf16[1,144,640]{2,1,0:T(8,128)(2,1)S(1)}, u32[]{:S(2)}, u32[]{:S(2)}) %collective-permute-start.31) | collective-permute-done | bytes 184352 | tf_op jit(solution)/shard_map/ppermute | solution.py:310
  89.9 2.6 %collective-permute-done.3.refs_4_ = bf16[1,144,640]{2,1,0:T(8,128)(2,1)S(1)} collective-permute-done((bf16[1,144,640]{2,1,0:T(8,128)(2,1)S(1)}, bf16[1,144,640]{2,1,0:T(8,128)(2,1)S(1)}, u32[]{:S(2)}, u32[]{:S(2)}) %collective-permute-start.3) | collective-permute-done | bytes 184352 | tf_op jit(solution)/shard_map/ppermute | solution.py:310
  92.5 1.5 collective-permute-start.20
  94.0 0.0 collective-permute-done.7.refs_8_
  94.0 0.5 collective-permute-start
  94.5 0.2 copy-done.12
  94.7 0.0 collective-permute-done.11.refs_12_
  94.7 0.0 all-to-all-done.2.refs_0_
  94.7 0.1 collective-permute-start.35
  94.8 8.3 %collective-permute-done.15.refs_16_ = bf16[1,144,640]{2,1,0:T(8,128)(2,1)} collective-permute-done((bf16[1,144,640]{2,1,0:T(8,128)(2,1)}, bf16[1,144,640]{2,1,0:T(8,128)(2,1)}, u32[]{:S(2)}, u32[]{:S(2)}) %collective-permute-start.15) | collective-permute-done | bytes 184352 | tf_op jit(solution)/shard_map/ppermute | solution.py:310
  103.1 0.0 collective-permute-start.25
  103.1 1.5 collective-permute-start.24
  104.6 0.2 collective-permute-start.29
  104.9 1.2 collective-permute-start.28
  106.0 13.8 %collective-permute-done.24.refs_5_ = bf16[1,144,640]{2,1,0:T(8,128)(2,1)} collective-permute-done((bf16[1,144,640]{2,1,0:T(8,128)(2,1)S(1)}, bf16[1,144,640]{2,1,0:T(8,128)(2,1)}, u32[]{:S(2)}, u32[]{:S(2)}) %collective-permute-start.24) | collective-permute-done | bytes 184352 | tf_op jit(solution)/shard_map/ppermute | solution.py:338
  119.9 1.5 collective-permute-start.32
  121.4 1.3 collective-permute-done.28.refs_9_
  122.7 1.5 collective-permute-start.4
  124.2 2.4 %collective-permute-done.32.refs_13_ = bf16[1,144,640]{2,1,0:T(8,128)(2,1)} collective-permute-done((bf16[1,144,640]{2,1,0:T(8,128)(2,1)}, bf16[1,144,640]{2,1,0:T(8,128)(2,1)}, u32[]{:S(2)}, u32[]{:S(2)}) %collective-permute-start.32) | collective-permute-done | bytes 184352 | tf_op jit(solution)/shard_map/ppermute | solution.py:338
  126.7 2.5 %collective-permute-start.8 = (bf16[1,144,640]{2,1,0:T(8,128)(2,1)}, bf16[1,144,640]{2,1,0:T(8,128)(2,1)S(1)}, u32[]{:S(2)}, u32[]{:S(2)}) collective-permute-start(bf16[1,144,640]{2,1,0:T(8,128)(2,1)} %copy-done.12), channel_id=1, source_target_pairs={{0,16},{8,24},{16,0},{24,8},{1,17},{9,25},{17,1},{25,9},{2,18},{10... | collective-permute-start | bytes 552968 | tf_op jit(solution)/shard_map/ppermute | solution.py:338
  129.2 0.3 collective-permute-done.4.refs_5_
  129.6 1.6 collective-permute-start.12
  131.2 3.8 %collective-permute-done.8.refs_9_ = bf16[1,144,640]{2,1,0:T(8,128)(2,1)S(1)} collective-permute-done((bf16[1,144,640]{2,1,0:T(8,128)(2,1)}, bf16[1,144,640]{2,1,0:T(8,128)(2,1)S(1)}, u32[]{:S(2)}, u32[]{:S(2)}) %collective-permute-start.8) | collective-permute-done | bytes 184352 | tf_op jit(solution)/shard_map/ppermute | solution.py:338
  134.9 0.5 collective-permute-start.2
  135.4 0.1 collective-permute-start.17
  135.5 3.1 %collective-permute-done.12.refs_13_ = bf16[1,144,640]{2,1,0:T(8,128)(2,1)S(1)} collective-permute-done((bf16[1,144,640]{2,1,0:T(8,128)(2,1)}, bf16[1,144,640]{2,1,0:T(8,128)(2,1)S(1)}, u32[]{:S(2)}, u32[]{:S(2)}) %collective-permute-start.12) | collective-permute-done | bytes 184352 | tf_op jit(solution)/shard_map/ppermute | solution.py:338
  138.6 1.7 collective-permute-start.16
  140.4 4.9 %collective-permute-done.16.refs_17_ = bf16[1,144,640]{2,1,0:T(8,128)(2,1)S(1)} collective-permute-done((bf16[1,144,640]{2,1,0:T(8,128)(2,1)}, bf16[1,144,640]{2,1,0:T(8,128)(2,1)S(1)}, u32[]{:S(2)}, u32[]{:S(2)}) %collective-permute-start.16) | collective-permute-done | bytes 184352 | tf_op jit(solution)/shard_map/ppermute | solution.py:338
  145.3 0.5 collective-permute-start.14
  145.8 0.9 collective-permute-done.10.refs_11_
  146.7 0.1 collective-permute-start.18
  146.8 0.1 collective-permute-done.14.refs_15_
  146.9 0.3 collective-permute-start.33
  147.2 0.9 collective-permute-done.18.refs_19_
  148.1 0.1 collective-permute-start.22
  148.3 0.4 collective-permute-start.26
  148.6 0.1 collective-permute-start.30
  148.8 0.4 collective-permute-start.34
  149.2 0.3 copy-done.10
  149.6 0.5 iota.3.row_ref
  150.1 19.5 %attend_some.1 = (bf16[8,192,512]{2,1,0:T(8,128)(2,1)}, bf16[8,192,512]{2,1,0:T(8,128)(2,1)}) custom-call(s32[7]{0:T(128)} %stack.31.meta_ref, s32[8,24]{1,0:T(8,128)} %bitcast.27, s32[8]{0:T(128)} %first_ref.3, s32[8]{0:T(128)} %accept_ref.1, s32[8]{0:T(128)} %iota.3.row_ref, bf16[4,144,640]{2,1,0:T(8,128)(2,1)} %all-to-all-done.1.refs_0_, ...), custom_call_target="tpu_custom_call" | custom-call | flops 4278190080 | bytes 11796480 | tf_op jit(solution)/shard_map/attend_some/pallas_call | solution.py:257
  169.6 2.8 %place_parts.2.refs_16_ = bf16[4,576,640]{2,1,0:T(8,128)(2,1)} custom-call(s32[7]{0:T(128)} %stack.31.meta_ref, s32[8,24]{1,0:T(8,128)} %bitcast.28, s32[8]{0:T(128)} %move_ref.5, bf16[4,288,640]{2,1,0:T(8,128)(2,1)} %copy-done, bf16[4,288,640]{2,1,0:T(8,128)(2,1)} %copy-done.1), custom_call_target="tpu_custom_call" | custom-call | flops 2949120 | bytes 2949120 | tf_op jit(solution)/shard_map/place_parts/pallas_call | solution.py:151
  172.5 3.5 %place_parts.3 = bf16[4,576,640]{2,1,0:T(8,128)(2,1)} custom-call(s32[7]{0:T(128)} %stack.31.meta_ref, s32[8,24]{1,0:T(8,128)} %bitcast.29, s32[8]{0:T(128)} %move_ref.5, bf16[1,144,640]{2,1,0:T(8,128)(2,1)} %copy-done.2, bf16[1,144,640]{2,1,0:T(8,128)(2,1)} %collective-permute-done.20.refs_1_, ...), custom_call_target="tpu_custom_call", output_to_operand_aliasing={{}: (19, {})} | custom-call | flops 2949120 | bytes 2949120 | tf_op jit(solution)/shard_map/place_parts/pallas_call | solution.py:151
  (86 shorter events, 0.2 us)
Async XLA Ops:
  1.9 13.7 %all-to-all-start = ((s32[8,1,24]{2,1,0:T(1,128)}), s32[8,1,24]{2,1,0:T(1,128)S(1)}, u32[]{:S(2)}, u32[]{:S(2)}) async-start(s32[8,1,24]{2,1,0:T(1,128)} %bitcast.30), calls=%async_computation | async-start | bytes 8192 | tf_op jit(solution)/shard_map/all_to_all | solution.py:313
  19.6 13.4 %all-to-all-start.1 = ((bf16[4,144,640]{2,1,0:T(8,128)(2,1)}), bf16[4,144,640]{2,1,0:T(8,128)(2,1)}, u32[]{:S(2)}, u32[]{:S(2)}) async-start(bf16[4,144,640]{2,1,0:T(8,128)(2,1)} %get-tuple-element.15), calls=%async_computation.1 | async-start | bytes 1474560 | tf_op jit(solution)/shard_map/all_to_all | solution.py:302
  27.4 9.1 %copy-start.31 = (bf16[1,144,640]{2,1,0:T(8,128)(2,1)S(1)}, bf16[1,144,640]{2,1,0:T(8,128)(2,1)}, u32[]{:S(2)}) copy-start(bf16[1,144,640]{2,1,0:T(8,128)(2,1)} %get-tuple-element.22) | copy-start | bytes 552964
  27.4 9.8 %copy-start.30 = (bf16[1,144,640]{2,1,0:T(8,128)(2,1)S(1)}, bf16[1,144,640]{2,1,0:T(8,128)(2,1)}, u32[]{:S(2)}) copy-start(bf16[1,144,640]{2,1,0:T(8,128)(2,1)} %get-tuple-element.23) | copy-start | bytes 552964
  27.5 13.5 %copy-start.29 = (bf16[1,144,640]{2,1,0:T(8,128)(2,1)S(1)}, bf16[1,144,640]{2,1,0:T(8,128)(2,1)}, u32[]{:S(2)}) copy-start(bf16[1,144,640]{2,1,0:T(8,128)(2,1)} %get-tuple-element.24) | copy-start | bytes 552964
  27.5 14.9 %copy-start.28 = (bf16[1,144,640]{2,1,0:T(8,128)(2,1)S(1)}, bf16[1,144,640]{2,1,0:T(8,128)(2,1)}, u32[]{:S(2)}) copy-start(bf16[1,144,640]{2,1,0:T(8,128)(2,1)} %get-tuple-element.25) | copy-start | bytes 552964
  27.5 18.2 %copy-start.23 = (bf16[1,144,640]{2,1,0:T(8,128)(2,1)S(1)}, bf16[1,144,640]{2,1,0:T(8,128)(2,1)}, u32[]{:S(2)}) copy-start(bf16[1,144,640]{2,1,0:T(8,128)(2,1)} %get-tuple-element.16) | copy-start | bytes 552964
  27.5 30.2 %copy-start.21 = (bf16[1,144,640]{2,1,0:T(8,128)(2,1)S(1)}, bf16[1,144,640]{2,1,0:T(8,128)(2,1)}, u32[]{:S(2)}) copy-start(bf16[1,144,640]{2,1,0:T(8,128)(2,1)} %get-tuple-element.17) | copy-start | bytes 552964
  27.5 39.0 %copy-start.19 = (bf16[1,144,640]{2,1,0:T(8,128)(2,1)S(1)}, bf16[1,144,640]{2,1,0:T(8,128)(2,1)}, u32[]{:S(2)}) copy-start(bf16[1,144,640]{2,1,0:T(8,128)(2,1)} %get-tuple-element.18) | copy-start | bytes 552964
  33.0 61.7 %all-to-all-start.2 = ((bf16[4,288,640]{2,1,0:T(8,128)(2,1)}), bf16[4,288,640]{2,1,0:T(8,128)(2,1)S(1)}, u32[]{:S(2)}, u32[]{:S(2)}) async-start(bf16[4,288,640]{2,1,0:T(8,128)(2,1)} %get-tuple-element.26), calls=%async_computation.2 | async-start | bytes 2949120 | tf_op jit(solution)/shard_map/all_to_all | solution.py:302
  36.6 21.1 %collective-permute-start.19 = (bf16[1,144,640]{2,1,0:T(8,128)(2,1)S(1)}, bf16[1,144,640]{2,1,0:T(8,128)(2,1)S(1)}, u32[]{:S(2)}, u32[]{:S(2)}) collective-permute-start(bf16[1,144,640]{2,1,0:T(8,128)(2,1)S(1)} %copy-done.31), channel_id=1, source_target_pairs={{0,4},{1,5},{2,6},{3,7},{4,0},{5,1},{6,2},{7,3},{8,12},{9,13},{10,... | collective-permute-start | bytes 552968 | tf_op jit(solution)/shard_map/ppermute | solution.py:310
  37.2 29.3 %collective-permute-start.23 = (bf16[1,144,640]{2,1,0:T(8,128)(2,1)S(1)}, bf16[1,144,640]{2,1,0:T(8,128)(2,1)S(1)}, u32[]{:S(2)}, u32[]{:S(2)}) collective-permute-start(bf16[1,144,640]{2,1,0:T(8,128)(2,1)S(1)} %copy-done.30), channel_id=1, source_target_pairs={{0,5},{1,6},{2,7},{3,4},{4,1},{5,2},{6,3},{7,0},{8,13},{9,14},{10,... | collective-permute-start | bytes 552968 | tf_op jit(solution)/shard_map/ppermute | solution.py:310
  40.9 27.9 %collective-permute-start.27 = (bf16[1,144,640]{2,1,0:T(8,128)(2,1)S(1)}, bf16[1,144,640]{2,1,0:T(8,128)(2,1)S(1)}, u32[]{:S(2)}, u32[]{:S(2)}) collective-permute-start(bf16[1,144,640]{2,1,0:T(8,128)(2,1)S(1)} %copy-done.29), channel_id=1, source_target_pairs={{0,6},{1,7},{2,4},{3,5},{4,2},{5,3},{6,0},{7,1},{8,14},{9,15},{10,... | collective-permute-start | bytes 552968 | tf_op jit(solution)/shard_map/ppermute | solution.py:310
  42.4 47.5 %collective-permute-start.31 = (bf16[1,144,640]{2,1,0:T(8,128)(2,1)S(1)}, bf16[1,144,640]{2,1,0:T(8,128)(2,1)S(1)}, u32[]{:S(2)}, u32[]{:S(2)}) collective-permute-start(bf16[1,144,640]{2,1,0:T(8,128)(2,1)S(1)} %copy-done.28), channel_id=1, source_target_pairs={{0,7},{1,4},{2,5},{3,6},{4,3},{5,0},{6,1},{7,2},{8,15},{9,12},{10,... | collective-permute-start | bytes 552968 | tf_op jit(solution)/shard_map/ppermute | solution.py:310
  45.7 46.8 %collective-permute-start.3 = (bf16[1,144,640]{2,1,0:T(8,128)(2,1)S(1)}, bf16[1,144,640]{2,1,0:T(8,128)(2,1)S(1)}, u32[]{:S(2)}, u32[]{:S(2)}) collective-permute-start(bf16[1,144,640]{2,1,0:T(8,128)(2,1)S(1)} %copy-done.23), channel_id=1, source_target_pairs={{0,4},{1,5},{2,6},{3,7},{4,0},{5,1},{6,2},{7,3},{8,12},{9,13},{10,... | collective-permute-start | bytes 552968 | tf_op jit(solution)/shard_map/ppermute | solution.py:310
  57.7 111.9 %copy-start.2 = (bf16[1,144,640]{2,1,0:T(8,128)(2,1)}, bf16[1,144,640]{2,1,0:T(8,128)(2,1)S(1)}, u32[]{:S(2)}) copy-start(bf16[1,144,640]{2,1,0:T(8,128)(2,1)S(1)} %collective-permute-done.19.refs_0_) | copy-start | bytes 552964
  57.7 36.3 %collective-permute-start.7 = (bf16[1,144,640]{2,1,0:T(8,128)(2,1)S(1)}, bf16[1,144,640]{2,1,0:T(8,128)(2,1)S(1)}, u32[]{:S(2)}, u32[]{:S(2)}) collective-permute-start(bf16[1,144,640]{2,1,0:T(8,128)(2,1)S(1)} %copy-done.21), channel_id=1, source_target_pairs={{0,5},{1,6},{2,7},{3,4},{4,1},{5,2},{6,3},{7,0},{8,13},{9,14},{10,... | collective-permute-start | bytes 552968 | tf_op jit(solution)/shard_map/ppermute | solution.py:310
  66.5 103.1 %copy-start.3 = (bf16[1,144,640]{2,1,0:T(8,128)(2,1)}, bf16[1,144,640]{2,1,0:T(8,128)(2,1)S(1)}, u32[]{:S(2)}) copy-start(bf16[1,144,640]{2,1,0:T(8,128)(2,1)S(1)} %collective-permute-done.23.refs_4_) | copy-start | bytes 552964
  66.5 28.2 %collective-permute-start.11 = (bf16[1,144,640]{2,1,0:T(8,128)(2,1)S(1)}, bf16[1,144,640]{2,1,0:T(8,128)(2,1)}, u32[]{:S(2)}, u32[]{:S(2)}) collective-permute-start(bf16[1,144,640]{2,1,0:T(8,128)(2,1)S(1)} %copy-done.19), channel_id=1, source_target_pairs={{0,6},{1,7},{2,4},{3,5},{4,2},{5,3},{6,0},{7,1},{8,14},{9,15},{10,... | collective-permute-start | bytes 552968 | tf_op jit(solution)/shard_map/ppermute | solution.py:310
  68.8 100.8 %copy-start.4 = (bf16[1,144,640]{2,1,0:T(8,128)(2,1)}, bf16[1,144,640]{2,1,0:T(8,128)(2,1)S(1)}, u32[]{:S(2)}) copy-start(bf16[1,144,640]{2,1,0:T(8,128)(2,1)S(1)} %collective-permute-done.27.refs_8_) | copy-start | bytes 552964
  68.8 34.3 %collective-permute-start.15 = (bf16[1,144,640]{2,1,0:T(8,128)(2,1)}, bf16[1,144,640]{2,1,0:T(8,128)(2,1)}, u32[]{:S(2)}, u32[]{:S(2)}) collective-permute-start(bf16[1,144,640]{2,1,0:T(8,128)(2,1)} %get-tuple-element.19), channel_id=1, source_target_pairs={{0,7},{1,4},{2,5},{3,6},{4,3},{5,0},{6,1},{7,2},{8,15},{9,12},{10,... | collective-permute-start | bytes 552968 | tf_op jit(solution)/shard_map/ppermute | solution.py:310
  89.9 4.7 %copy-start.5 = (bf16[1,144,640]{2,1,0:T(8,128)(2,1)}, bf16[1,144,640]{2,1,0:T(8,128)(2,1)S(1)}, u32[]{:S(2)}) copy-start(bf16[1,144,640]{2,1,0:T(8,128)(2,1)S(1)} %collective-permute-done.31.refs_12_) | copy-start | bytes 552964
  89.9 13.2 %collective-permute-start.21 = (bf16[1,144,640]{2,1,0:T(8,128)(2,1)S(1)}, bf16[1,144,640]{2,1,0:T(8,128)(2,1)}, u32[]{:S(2)}, u32[]{:S(2)}) collective-permute-start(bf16[1,144,640]{2,1,0:T(8,128)(2,1)S(1)} %collective-permute-done.19.refs_0_), channel_id=1, source_target_pairs={{0,8},{8,0},{16,24},{24,16},{1,9},{9,1},{17,25},{25,17},{2,10},{10... | collective-permute-start | bytes 552968 | tf_op jit(solution)/shard_map/ppermute | solution.py:340
  92.5 12.1 %collective-permute-start.20 = (bf16[1,144,640]{2,1,0:T(8,128)(2,1)S(1)}, bf16[1,144,640]{2,1,0:T(8,128)(2,1)}, u32[]{:S(2)}, u32[]{:S(2)}) collective-permute-start(bf16[1,144,640]{2,1,0:T(8,128)(2,1)S(1)} %collective-permute-done.19.refs_0_), channel_id=1, source_target_pairs={{0,16},{8,24},{16,0},{24,8},{1,17},{9,25},{17,1},{25,9},{2,18},{10... | collective-permute-start | bytes 552968 | tf_op jit(solution)/shard_map/ppermute | solution.py:338
  94.0 40.9 %collective-permute-start = (bf16[4,144,640]{2,1,0:T(8,128)(2,1)}, bf16[4,144,640]{2,1,0:T(8,128)(2,1)}, u32[]{:S(2)}, u32[]{:S(2)}) collective-permute-start(bf16[4,144,640]{2,1,0:T(8,128)(2,1)} %all-to-all-done.1.refs_0_), channel_id=1, source_target_pairs={{0,16},{8,24},{16,0},{24,8},{1,17},{9,25},{17,1},{25,9},{2,18},{10... | collective-permute-start | bytes 2211848 | tf_op jit(solution)/shard_map/ppermute | solution.py:338
  94.7 74.9 %copy-start = (bf16[4,288,640]{2,1,0:T(8,128)(2,1)}, bf16[4,288,640]{2,1,0:T(8,128)(2,1)S(1)}, u32[]{:S(2)}) copy-start(bf16[4,288,640]{2,1,0:T(8,128)(2,1)S(1)} %all-to-all-done.2.refs_0_) | copy-start | bytes 4423684
  94.7 54.1 %collective-permute-start.35 = (bf16[4,288,640]{2,1,0:T(8,128)(2,1)S(1)}, bf16[4,288,640]{2,1,0:T(8,128)(2,1)S(1)}, u32[]{:S(2)}, u32[]{:S(2)}) collective-permute-start(bf16[4,288,640]{2,1,0:T(8,128)(2,1)S(1)} %all-to-all-done.2.refs_0_), channel_id=1, source_target_pairs={{0,8},{8,0},{16,24},{24,16},{1,9},{9,1},{17,25},{25,17},{2,10},{10... | collective-permute-start | bytes 4423688 | tf_op jit(solution)/shard_map/ppermute | solution.py:379
  103.1 1.8 %collective-permute-start.25 = (bf16[1,144,640]{2,1,0:T(8,128)(2,1)S(1)}, bf16[1,144,640]{2,1,0:T(8,128)(2,1)S(1)}, u32[]{:S(2)}, u32[]{:S(2)}) collective-permute-start(bf16[1,144,640]{2,1,0:T(8,128)(2,1)S(1)} %collective-permute-done.23.refs_4_), channel_id=1, source_target_pairs={{0,8},{8,0},{16,24},{24,16},{1,9},{9,1},{17,25},{25,17},{2,10},{10... | collective-permute-start | bytes 552968 | tf_op jit(solution)/shard_map/ppermute | solution.py:340
  103.1 16.8 %collective-permute-start.24 = (bf16[1,144,640]{2,1,0:T(8,128)(2,1)S(1)}, bf16[1,144,640]{2,1,0:T(8,128)(2,1)}, u32[]{:S(2)}, u32[]{:S(2)}) collective-permute-start(bf16[1,144,640]{2,1,0:T(8,128)(2,1)S(1)} %collective-permute-done.23.refs_4_), channel_id=1, source_target_pairs={{0,16},{8,24},{16,0},{24,8},{1,17},{9,25},{17,1},{25,9},{2,18},{10... | collective-permute-start | bytes 552968 | tf_op jit(solution)/shard_map/ppermute | solution.py:338
  104.6 16.8 %collective-permute-start.29 = (bf16[1,144,640]{2,1,0:T(8,128)(2,1)S(1)}, bf16[1,144,640]{2,1,0:T(8,128)(2,1)S(1)}, u32[]{:S(2)}, u32[]{:S(2)}) collective-permute-start(bf16[1,144,640]{2,1,0:T(8,128)(2,1)S(1)} %collective-permute-done.27.refs_8_), channel_id=1, source_target_pairs={{0,8},{8,0},{16,24},{24,16},{1,9},{9,1},{17,25},{25,17},{2,10},{10... | collective-permute-start | bytes 552968 | tf_op jit(solution)/shard_map/ppermute | solution.py:340
  104.9 43.9 %copy-start.6 = (bf16[1,144,640]{2,1,0:T(8,128)(2,1)}, bf16[1,144,640]{2,1,0:T(8,128)(2,1)S(1)}, u32[]{:S(2)}) copy-start(bf16[1,144,640]{2,1,0:T(8,128)(2,1)S(1)} %collective-permute-done.25.refs_6_) | copy-start | bytes 552964
  104.9 17.9 %collective-permute-start.28 = (bf16[1,144,640]{2,1,0:T(8,128)(2,1)S(1)}, bf16[1,144,640]{2,1,0:T(8,128)(2,1)}, u32[]{:S(2)}, u32[]{:S(2)}) collective-permute-start(bf16[1,144,640]{2,1,0:T(8,128)(2,1)S(1)} %collective-permute-done.27.refs_8_), channel_id=1, source_target_pairs={{0,16},{8,24},{16,0},{24,8},{1,17},{9,25},{17,1},{25,9},{2,18},{10... | collective-permute-start | bytes 552968 | tf_op jit(solution)/shard_map/ppermute | solution.py:338
  119.9 6.8 %collective-permute-start.32 = (bf16[1,144,640]{2,1,0:T(8,128)(2,1)}, bf16[1,144,640]{2,1,0:T(8,128)(2,1)}, u32[]{:S(2)}, u32[]{:S(2)}) collective-permute-start(bf16[1,144,640]{2,1,0:T(8,128)(2,1)} %copy-done.5), channel_id=1, source_target_pairs={{0,16},{8,24},{16,0},{24,8},{1,17},{9,25},{17,1},{25,9},{2,18},{10... | collective-permute-start | bytes 552968 | tf_op jit(solution)/shard_map/ppermute | solution.py:338
  121.4 27.8 %copy-start.7 = (bf16[1,144,640]{2,1,0:T(8,128)(2,1)}, bf16[1,144,640]{2,1,0:T(8,128)(2,1)S(1)}, u32[]{:S(2)}) copy-start(bf16[1,144,640]{2,1,0:T(8,128)(2,1)S(1)} %collective-permute-done.29.refs_10_) | copy-start | bytes 552964
  121.4 5.3 %collective-permute-start.5 = (bf16[1,144,640]{2,1,0:T(8,128)(2,1)}, bf16[1,144,640]{2,1,0:T(8,128)(2,1)S(1)}, u32[]{:S(2)}, u32[]{:S(2)}) collective-permute-start(bf16[1,144,640]{2,1,0:T(8,128)(2,1)} %copy-done.11), channel_id=1, source_target_pairs={{0,8},{8,0},{16,24},{24,16},{1,9},{9,1},{17,25},{25,17},{2,10},{10... | collective-permute-start | bytes 552968 | tf_op jit(solution)/shard_map/ppermute | solution.py:340
  122.7 6.8 %collective-permute-start.4 = (bf16[1,144,640]{2,1,0:T(8,128)(2,1)}, bf16[1,144,640]{2,1,0:T(8,128)(2,1)S(1)}, u32[]{:S(2)}, u32[]{:S(2)}) collective-permute-start(bf16[1,144,640]{2,1,0:T(8,128)(2,1)} %copy-done.11), channel_id=1, source_target_pairs={{0,16},{8,24},{16,0},{24,8},{1,17},{9,25},{17,1},{25,9},{2,18},{10... | collective-permute-start | bytes 552968 | tf_op jit(solution)/shard_map/ppermute | solution.py:338
  126.7 2.9 %collective-permute-start.9 = (bf16[1,144,640]{2,1,0:T(8,128)(2,1)}, bf16[1,144,640]{2,1,0:T(8,128)(2,1)S(1)}, u32[]{:S(2)}, u32[]{:S(2)}) collective-permute-start(bf16[1,144,640]{2,1,0:T(8,128)(2,1)} %copy-done.12), channel_id=1, source_target_pairs={{0,8},{8,0},{16,24},{24,16},{1,9},{9,1},{17,25},{25,17},{2,10},{10... | collective-permute-start | bytes 552968 | tf_op jit(solution)/shard_map/ppermute | solution.py:340
  126.7 4.5 %copy-start.13 = (bf16[1,144,640]{2,1,0:T(8,128)(2,1)}, bf16[1,144,640]{2,1,0:T(8,128)(2,1)S(1)}, u32[]{:S(2)}) copy-start(bf16[1,144,640]{2,1,0:T(8,128)(2,1)S(1)} %collective-permute-done.5.refs_6_) | copy-start | bytes 552964
  126.7 8.2 %collective-permute-start.8 = (bf16[1,144,640]{2,1,0:T(8,128)(2,1)}, bf16[1,144,640]{2,1,0:T(8,128)(2,1)S(1)}, u32[]{:S(2)}, u32[]{:S(2)}) collective-permute-start(bf16[1,144,640]{2,1,0:T(8,128)(2,1)} %copy-done.12), channel_id=1, source_target_pairs={{0,16},{8,24},{16,0},{24,8},{1,17},{9,25},{17,1},{25,9},{2,18},{10... | collective-permute-start | bytes 552968 | tf_op jit(solution)/shard_map/ppermute | solution.py:338
  129.6 19.9 %copy-start.14 = (bf16[1,144,640]{2,1,0:T(8,128)(2,1)}, bf16[1,144,640]{2,1,0:T(8,128)(2,1)S(1)}, u32[]{:S(2)}) copy-start(bf16[1,144,640]{2,1,0:T(8,128)(2,1)S(1)} %collective-permute-done.4.refs_5_) | copy-start | bytes 552964
  129.6 5.9 %collective-permute-start.13 = (bf16[1,144,640]{2,1,0:T(8,128)(2,1)}, bf16[1,144,640]{2,1,0:T(8,128)(2,1)S(1)}, u32[]{:S(2)}, u32[]{:S(2)}) collective-permute-start(bf16[1,144,640]{2,1,0:T(8,128)(2,1)} %collective-permute-done.11.refs_12_), channel_id=1, source_target_pairs={{0,8},{8,0},{16,24},{24,16},{1,9},{9,1},{17,25},{25,17},{2,10},{10... | collective-permute-start | bytes 552968 | tf_op jit(solution)/shard_map/ppermute | solution.py:340
  129.6 9.0 %collective-permute-start.12 = (bf16[1,144,640]{2,1,0:T(8,128)(2,1)}, bf16[1,144,640]{2,1,0:T(8,128)(2,1)S(1)}, u32[]{:S(2)}, u32[]{:S(2)}) collective-permute-start(bf16[1,144,640]{2,1,0:T(8,128)(2,1)} %collective-permute-done.11.refs_12_), channel_id=1, source_target_pairs={{0,16},{8,24},{16,0},{24,8},{1,17},{9,25},{17,1},{25,9},{2,18},{10... | collective-permute-start | bytes 552968 | tf_op jit(solution)/shard_map/ppermute | solution.py:338
  134.9 14.6 %copy-start.16 = (bf16[1,144,640]{2,1,0:T(8,128)(2,1)}, bf16[1,144,640]{2,1,0:T(8,128)(2,1)S(1)}, u32[]{:S(2)}) copy-start(bf16[1,144,640]{2,1,0:T(8,128)(2,1)S(1)} %collective-permute-done.8.refs_9_) | copy-start | bytes 552964
  134.9 13.3 %collective-permute-start.1 = (bf16[4,144,640]{2,1,0:T(8,128)(2,1)}, bf16[4,144,640]{2,1,0:T(8,128)(2,1)S(1)}, u32[]{:S(2)}, u32[]{:S(2)}) collective-permute-start(bf16[4,144,640]{2,1,0:T(8,128)(2,1)} %all-to-all-done.1.refs_0_), channel_id=1, source_target_pairs={{0,8},{8,0},{16,24},{24,16},{1,9},{9,1},{17,25},{25,17},{2,10},{10... | collective-permute-start | bytes 2211848 | tf_op jit(solution)/shard_map/ppermute | solution.py:340
  134.9 13.7 %collective-permute-start.2 = (bf16[4,144,640]{2,1,0:T(8,128)(2,1)}, bf16[4,144,640]{2,1,0:T(8,128)(2,1)S(1)}, u32[]{:S(2)}, u32[]{:S(2)}) collective-permute-start(bf16[4,144,640]{2,1,0:T(8,128)(2,1)} %collective-permute-done.refs_1_), channel_id=1, source_target_pairs={{0,8},{8,0},{16,24},{24,16},{1,9},{9,1},{17,25},{25,17},{2,10},{10... | collective-permute-start | bytes 2211848 | tf_op jit(solution)/shard_map/ppermute | solution.py:340
  135.4 14.0 %copy-start.17 = (bf16[1,144,640]{2,1,0:T(8,128)(2,1)}, bf16[1,144,640]{2,1,0:T(8,128)(2,1)S(1)}, u32[]{:S(2)}) copy-start(bf16[1,144,640]{2,1,0:T(8,128)(2,1)S(1)} %collective-permute-done.13.refs_14_) | copy-start | bytes 552964
  135.4 4.9 %collective-permute-start.17 = (bf16[1,144,640]{2,1,0:T(8,128)(2,1)}, bf16[1,144,640]{2,1,0:T(8,128)(2,1)S(1)}, u32[]{:S(2)}, u32[]{:S(2)}) collective-permute-start(bf16[1,144,640]{2,1,0:T(8,128)(2,1)} %collective-permute-done.15.refs_16_), channel_id=1, source_target_pairs={{0,8},{8,0},{16,24},{24,16},{1,9},{9,1},{17,25},{25,17},{2,10},{10... | collective-permute-start | bytes 552968 | tf_op jit(solution)/shard_map/ppermute | solution.py:340
  138.6 10.9 %copy-start.18 = (bf16[1,144,640]{2,1,0:T(8,128)(2,1)}, bf16[1,144,640]{2,1,0:T(8,128)(2,1)S(1)}, u32[]{:S(2)}) copy-start(bf16[1,144,640]{2,1,0:T(8,128)(2,1)S(1)} %collective-permute-done.12.refs_13_) | copy-start | bytes 552964
  138.6 6.6 %collective-permute-start.16 = (bf16[1,144,640]{2,1,0:T(8,128)(2,1)}, bf16[1,144,640]{2,1,0:T(8,128)(2,1)S(1)}, u32[]{:S(2)}, u32[]{:S(2)}) collective-permute-start(bf16[1,144,640]{2,1,0:T(8,128)(2,1)} %collective-permute-done.15.refs_16_), channel_id=1, source_target_pairs={{0,16},{8,24},{16,0},{24,8},{1,17},{9,25},{17,1},{25,9},{2,18},{10... | collective-permute-start | bytes 552968 | tf_op jit(solution)/shard_map/ppermute | solution.py:338
  140.4 9.1 %copy-start.20 = (bf16[1,144,640]{2,1,0:T(8,128)(2,1)}, bf16[1,144,640]{2,1,0:T(8,128)(2,1)S(1)}, u32[]{:S(2)}) copy-start(bf16[1,144,640]{2,1,0:T(8,128)(2,1)S(1)} %collective-permute-done.17.refs_18_) | copy-start | bytes 552964
  140.4 4.9 %collective-permute-start.6 = (bf16[1,144,640]{2,1,0:T(8,128)(2,1)S(1)}, bf16[1,144,640]{2,1,0:T(8,128)(2,1)S(1)}, u32[]{:S(2)}, u32[]{:S(2)}) collective-permute-start(bf16[1,144,640]{2,1,0:T(8,128)(2,1)S(1)} %collective-permute-done.4.refs_5_), channel_id=1, source_target_pairs={{0,8},{8,0},{16,24},{24,16},{1,9},{9,1},{17,25},{25,17},{2,10},{10... | collective-permute-start | bytes 552968 | tf_op jit(solution)/shard_map/ppermute | solution.py:340
  145.2 4.3 %copy-start.22 = (bf16[1,144,640]{2,1,0:T(8,128)(2,1)}, bf16[1,144,640]{2,1,0:T(8,128)(2,1)S(1)}, u32[]{:S(2)}) copy-start(bf16[1,144,640]{2,1,0:T(8,128)(2,1)S(1)} %collective-permute-done.16.refs_17_) | copy-start | bytes 552964
  145.3 1.4 collective-permute-start.10
  145.3 4.3 %copy-start.24 = (bf16[1,144,640]{2,1,0:T(8,128)(2,1)}, bf16[1,144,640]{2,1,0:T(8,128)(2,1)S(1)}, u32[]{:S(2)}) copy-start(bf16[1,144,640]{2,1,0:T(8,128)(2,1)S(1)} %collective-permute-done.6.refs_7_) | copy-start | bytes 552964
  145.3 1.7 collective-permute-start.14
  146.7 2.9 %copy-start.25 = (bf16[1,144,640]{2,1,0:T(8,128)(2,1)}, bf16[1,144,640]{2,1,0:T(8,128)(2,1)S(1)}, u32[]{:S(2)}) copy-start(bf16[1,144,640]{2,1,0:T(8,128)(2,1)S(1)} %collective-permute-done.10.refs_11_) | copy-start | bytes 552964
  146.7 1.4 collective-permute-start.18
  146.9 2.6 %copy-start.26 = (bf16[1,144,640]{2,1,0:T(8,128)(2,1)}, bf16[1,144,640]{2,1,0:T(8,128)(2,1)S(1)}, u32[]{:S(2)}) copy-start(bf16[1,144,640]{2,1,0:T(8,128)(2,1)S(1)} %collective-permute-done.14.refs_15_) | copy-start | bytes 552964
  146.9 25.5 %collective-permute-start.33 = (bf16[1,144,640]{2,1,0:T(8,128)(2,1)}, bf16[1,144,640]{2,1,0:T(8,128)(2,1)}, u32[]{:S(2)}, u32[]{:S(2)}) collective-permute-start(bf16[1,144,640]{2,1,0:T(8,128)(2,1)} %copy-done.5), channel_id=1, source_target_pairs={{0,8},{8,0},{16,24},{24,16},{1,9},{9,1},{17,25},{25,17},{2,10},{10... | collective-permute-start | bytes 552968 | tf_op jit(solution)/shard_map/ppermute | solution.py:340
  148.1 24.3 %collective-permute-start.22 = (bf16[1,144,640]{2,1,0:T(8,128)(2,1)}, bf16[1,144,640]{2,1,0:T(8,128)(2,1)}, u32[]{:S(2)}, u32[]{:S(2)}) collective-permute-start(bf16[1,144,640]{2,1,0:T(8,128)(2,1)} %collective-permute-done.20.refs_1_), channel_id=1, source_target_pairs={{0,8},{8,0},{16,24},{24,16},{1,9},{9,1},{17,25},{25,17},{2,10},{10... | collective-permute-start | bytes 552968 | tf_op jit(solution)/shard_map/ppermute | solution.py:340
  148.3 24.2 %collective-permute-start.26 = (bf16[1,144,640]{2,1,0:T(8,128)(2,1)}, bf16[1,144,640]{2,1,0:T(8,128)(2,1)}, u32[]{:S(2)}, u32[]{:S(2)}) collective-permute-start(bf16[1,144,640]{2,1,0:T(8,128)(2,1)} %collective-permute-done.24.refs_5_), channel_id=1, source_target_pairs={{0,8},{8,0},{16,24},{24,16},{1,9},{9,1},{17,25},{25,17},{2,10},{10... | collective-permute-start | bytes 552968 | tf_op jit(solution)/shard_map/ppermute | solution.py:340
  148.6 23.8 %collective-permute-start.30 = (bf16[1,144,640]{2,1,0:T(8,128)(2,1)}, bf16[1,144,640]{2,1,0:T(8,128)(2,1)}, u32[]{:S(2)}, u32[]{:S(2)}) collective-permute-start(bf16[1,144,640]{2,1,0:T(8,128)(2,1)} %collective-permute-done.28.refs_9_), channel_id=1, source_target_pairs={{0,8},{8,0},{16,24},{24,16},{1,9},{9,1},{17,25},{25,17},{2,10},{10... | collective-permute-start | bytes 552968 | tf_op jit(solution)/shard_map/ppermute | solution.py:340
  148.8 20.9 %copy-start.1 = (bf16[4,288,640]{2,1,0:T(8,128)(2,1)}, bf16[4,288,640]{2,1,0:T(8,128)(2,1)S(1)}, u32[]{:S(2)}) copy-start(bf16[4,288,640]{2,1,0:T(8,128)(2,1)S(1)} %collective-permute-done.35.refs_1_) | copy-start | bytes 4423684
  148.8 23.7 %collective-permute-start.34 = (bf16[1,144,640]{2,1,0:T(8,128)(2,1)}, bf16[1,144,640]{2,1,0:T(8,128)(2,1)}, u32[]{:S(2)}, u32[]{:S(2)}) collective-permute-start(bf16[1,144,640]{2,1,0:T(8,128)(2,1)} %collective-permute-done.32.refs_13_), channel_id=1, source_target_pairs={{0,8},{8,0},{16,24},{24,16},{1,9},{9,1},{17,25},{25,17},{2,10},{10... | collective-permute-start | bytes 552968 | tf_op jit(solution)/shard_map/ppermute | solution.py:340
  (7 other events, 8.2 us)
